TPU v7x, 256 devices: a whole 4x4x8 slice. The times are simulated.
256 devices in a mesh: slab: 128 (over y, x, z_hi, core), cell: 2 (over z_lo).
Axes of the slice: x: 4, y: 4, z: 8 (z_hi: 4, z_lo: 2; z = z_hi * 2 + z_lo), core: 2. Of those that a mesh axis runs over, the one named last changes fastest.
Arguments:
- cell_row: int32 [131072], P(('slab', 'cell')), may hold values from 0 to 2043, as said below
- cell_col: int32 [131072], P(('slab', 'cell')), may hold values from 0 to 2039
- cell_width: int32 [131072], P(('slab', 'cell')), may hold values from 1 to 8
- cell_height: int32 [131072], P(('slab', 'cell')), may hold values from 1 to 4
- cell_region: int32 [131072], P(('slab', 'cell')), may hold values from 0 to 3
- cell_offset: float32 [2, 131072], P(None, ('slab', 'cell')), may hold values from 0 to 1
Outputs:
- field_x: float32 [4, 2048, 2048], P(None, ('slab', 'cell'))
- field_y: float32 [4, 2048, 2048], P(None, ('slab', 'cell'))
- cell_force: float32 [2, 131072], P(None, ('slab', 'cell'))
- energy: float32 [], replicated
- overflow: float32 [], replicated
Inputs may be any that keep to these rules, and one draw needn't show every extreme that they name: `cell_row`: cell i belongs to row slab s = i // 1024: its row lies in [s * 16, (s + 1) * 16); cells of the last slab lie at least 4 rows below the top of the grid.
All inputs are finite; a program needn't handle non-finite values.
Results may differ from a plain program's by a relative error of at most 0.0015.
Values may be sent and summed in bfloat16 or wider, within the bound.
A program may use at most 128 MiB of HBM per device.

v0:
```python
import math

import jax
import jax.numpy as jnp
from jax import lax
from jax.sharding import Mesh
from jax.sharding import PartitionSpec as P

M = 2048
REGIONS = 4
HMAX = 4
SLAB = ("slab_0", "slab_1", "slab_2", "slab_3")
SLAB_CELL = ("slab_0", "slab_1", "slab_2", "slab_3", "cell")


def shifted(value, axis, steps):
    count = lax.axis_size(axis)
    first, last = (max(0, -steps), min(count, count - steps))
    return lax.ppermute(value, axis, [(source, source + steps) for source in range(first, last)])


def cut_along(shard, dim, length):
    before, after = (shard.shape[:dim], shard.shape[dim + 1 :])
    return jnp.moveaxis(shard.reshape(*before, length, -1, *after), dim, 0)


def sent_and_summed(shard, axis, dim):
    length = lax.axis_size(axis)
    pieces = lax.all_to_all(cut_along(shard, dim, length), axis, 0, 0, tiled=True)
    return jnp.sum(pieces, axis=0)


def joined_along(pieces, dim):
    dims = list(pieces.shape[1:])
    dims[dim] *= pieces.shape[0]
    return jnp.moveaxis(pieces, 0, dim).reshape(dims)


def one_exchange(shard, axis, axes, splits, concats):
    sizes = [lax.axis_size(a) for a in axes]
    pieces = cut_along(shard, splits[0], sizes[0])
    pieces = jnp.moveaxis(cut_along(pieces, splits[1] + 1, sizes[1]), 0, 1)
    inside = pieces.shape[2:]
    pieces = pieces.reshape(-1, *inside)
    pieces = lax.all_to_all(pieces, axis, split_axis=0, concat_axis=0, tiled=True)
    pieces = joined_along(pieces.reshape(*sizes, *inside), concats[0] + 1)
    return joined_along(pieces, concats[1])


def from_everyone(shard, axis):
    copies = jnp.broadcast_to(shard, (lax.axis_size(axis), *shard.shape))
    return lax.all_to_all(copies, axis, split_axis=0, concat_axis=0, tiled=True)


def gathered_copies(shard, axis, dim):
    return joined_along(from_everyone(shard, axis), dim)


def one_axis_at_a_time(shard, axes):
    for axis in axes:
        shard = lax.psum(shard, axis)
    return shard


def intersect(offset_bins, fraction, extent):
    high_edge = jnp.minimum(offset_bins + 1.0, fraction + extent)
    low_edge = jnp.maximum(offset_bins, fraction)
    return jnp.maximum(high_edge - low_edge, 0.0).astype(jnp.bfloat16)


def basis_tables(length):
    freq_col = lax.iota(jnp.int32, length)[:, None]
    pos_row = lax.iota(jnp.int32, length)[None, :]
    phase_int = freq_col * (2 * pos_row + 1) % (4 * length)
    angle_grid = phase_int.astype(jnp.float32) * (math.pi / (2.0 * length))
    weight = jnp.where(freq_col == 0, math.sqrt(1.0 / length), math.sqrt(2.0 / length)).astype(
        jnp.float32
    )
    return (weight * jnp.cos(angle_grid), weight * jnp.sin(angle_grid))


def transform(source, contract, table, freq_out):
    table_dim = 1 if freq_out else 0
    return lax.dot_general(
        source,
        table,
        (((contract,), (table_dim,)), ((), ())),
        precision=lax.Precision.HIGHEST,
        preferred_element_type=jnp.float32,
    )


def natural_order(values, slab_count, cell_count):
    lead = values.shape[0]
    total_len = values.shape[1]
    tail = values.shape[2]
    width = total_len // (slab_count * cell_count)
    shaped = values.reshape(lead, cell_count, slab_count, width, tail)
    return jnp.swapaxes(shaped, 1, 2).reshape(lead, total_len, tail)


def body(cell_row, cell_col, cell_width, cell_height, cell_region, cell_offset):
    slab_count = lax.axis_size(SLAB)
    cell_count = lax.axis_size("cell")
    slab_index = lax.axis_index(SLAB)
    cell_index = lax.axis_index("cell")
    length = M
    regions = REGIONS
    spill_rows = HMAX
    slab_rows = length // slab_count
    extended = slab_rows + spill_rows
    block_width = length // (slab_count * cell_count)
    cell_total = cell_row.shape[0]
    group_size = math.gcd(cell_total, 256)
    group_count = cell_total // group_size
    base_row = slab_index * slab_rows
    natural = lax.iota(jnp.int32, length)
    cosine, sine_table = basis_tables(length)

    def profiles(group_index):
        start = group_index * group_size
        rows_here = lax.dynamic_slice_in_dim(cell_row, start, group_size)
        cols_here = lax.dynamic_slice_in_dim(cell_col, start, group_size)
        widths_here = lax.dynamic_slice_in_dim(cell_width, start, group_size).astype(jnp.float32)
        heights_here = lax.dynamic_slice_in_dim(cell_height, start, group_size).astype(jnp.float32)
        regions_here = lax.dynamic_slice_in_dim(cell_region, start, group_size)
        offsets_here = lax.dynamic_slice_in_dim(cell_offset, start, group_size, 1)
        x_bins = (natural[None, :] - cols_here[:, None]).astype(jnp.float32)
        x_intersect = intersect(x_bins, offsets_here[0][:, None], widths_here[:, None])
        y_bins = (base_row + lax.iota(jnp.int32, extended)[None, :] - rows_here[:, None]).astype(
            jnp.float32
        )
        y_intersect = intersect(y_bins, offsets_here[1][:, None], heights_here[:, None])
        region_hot = (regions_here[:, None] == lax.iota(jnp.int32, regions)[None, :]).astype(
            jnp.bfloat16
        )
        y_region = (y_intersect[:, None, :] * region_hot[:, :, None]).reshape(
            group_size, regions * extended
        )
        return (x_intersect, y_region)

    def add_density(group_index, running):
        x_intersect, y_region = profiles(group_index)
        return running + lax.dot_general(
            y_region, x_intersect, (((0,), (0,)), ((), ())), preferred_element_type=jnp.float32
        )

    density_ext = lax.fori_loop(
        0, group_count, add_density, jnp.zeros((regions * extended, length), jnp.float32)
    )
    density_ext = density_ext.reshape(regions, extended, length)
    arriving = shifted(density_ext[:, slab_rows:, :].astype(jnp.bfloat16), SLAB, 1).astype(
        jnp.float32
    )
    slab_density = jnp.concatenate(
        [density_ext[:, :spill_rows, :] + arriving, density_ext[:, spill_rows:slab_rows, :]], axis=1
    )
    density = sent_and_summed(slab_density, "cell", 1)
    excess_local = jnp.sum(jnp.maximum(density - 1.0, 0.0))
    area_local = jnp.sum(density)
    by_freq_x = transform(density, 2, cosine, True)
    crossed = lax.all_to_all(
        lax.all_to_all(by_freq_x, SLAB, split_axis=2, concat_axis=1, tiled=True),
        "cell",
        split_axis=2,
        concat_axis=1,
        tiled=True,
    )
    spectrum = transform(natural_order(crossed, slab_count, cell_count), 1, cosine, True)
    kx_values = (slab_index * cell_count + cell_index) * block_width + lax.iota(
        jnp.int32, block_width
    )
    kx_float = kx_values.astype(jnp.float32)[:, None]
    ky_float = natural.astype(jnp.float32)[None, :]
    at_anchor = kx_values[:, None] + natural[None, :] == 0
    step_size = math.pi / length
    squared = kx_float * kx_float + ky_float * ky_float
    potential_hat = jnp.where(
        at_anchor, 0.0, spectrum / (step_size * step_size * jnp.where(at_anchor, 1.0, squared))
    )
    drive_x = potential_hat * (step_size * kx_float)
    drive_y = potential_hat * (step_size * ky_float)
    along_x = transform(drive_x, 2, cosine, False)
    along_y = transform(drive_y, 2, sine_table, False)
    back_x, back_y = (
        one_exchange(along_x, SLAB_CELL, (SLAB, "cell"), (2, 2), (1, 1)),
        one_exchange(along_y, SLAB_CELL, (SLAB, "cell"), (2, 2), (1, 1)),
    )
    field_x = transform(natural_order(back_x, slab_count, cell_count), 1, sine_table, False)
    field_y = transform(natural_order(back_y, slab_count, cell_count), 1, cosine, False)
    energy_local = jnp.sum(spectrum * potential_hat) / (length * length)
    rounded = jnp.concatenate([field_x.astype(jnp.bfloat16), field_y.astype(jnp.bfloat16)], axis=0)
    whole_slab = gathered_copies(rounded, "cell", 1)
    from_above = shifted(whole_slab[:, :spill_rows, :], SLAB, -1)
    field_ext = jnp.concatenate([whole_slab, from_above], axis=1).reshape(
        2 * regions * extended, length
    )

    def one_force(group_index, forces):
        x_intersect, y_region = profiles(group_index)
        sampled = lax.dot_general(
            x_intersect, field_ext, (((1,), (1,)), ((), ())), preferred_element_type=jnp.float32
        )
        sampled = sampled.reshape(group_size, 2, regions * extended)
        pushed = jnp.sum(sampled * y_region.astype(jnp.float32)[:, None, :], axis=2)
        return lax.dynamic_update_slice_in_dim(forces, pushed.T, group_index * group_size, 1)

    cell_force = lax.fori_loop(0, group_count, one_force, jnp.zeros((2, cell_total), jnp.float32))
    excess, area, energy = (
        one_axis_at_a_time(excess_local, SLAB_CELL),
        one_axis_at_a_time(area_local, SLAB_CELL),
        one_axis_at_a_time(energy_local, SLAB_CELL),
    )
    overflow = excess / area
    return (field_x, field_y, cell_force, energy, overflow)


def solution(mesh):
    finer = Mesh(
        mesh.devices.reshape(4, 4, 4, 2, mesh.shape["cell"]),
        ("slab_0", "slab_1", "slab_2", "slab_3", "cell"),
    )
    placed = (
        P(SLAB_CELL),
        P(SLAB_CELL),
        P(SLAB_CELL),
        P(SLAB_CELL),
        P(SLAB_CELL),
        P(None, SLAB_CELL),
    )
    return jax.shard_map(
        body,
        mesh=finer,
        in_specs=placed,
        out_specs=(
            P(None, SLAB_CELL, None),
            P(None, SLAB_CELL, None),
            P(None, SLAB_CELL),
            P(),
            P(),
        ),
        check_vma=False,
    )
```

profile of v0, /device:TPU:1, one launch (start us, length us, event | category | flops | bytes accessed | tf_op | source)
XLA Modules:
  0.0 732.3 jit_solution(15791731992356647391)
XLA Ops:
  0.7 9.8 %while.29 = (s32[]{:T(128)}, f32[80,2048]{1,0:T(8,128)S(1)}, s32[]{:T(128)}, s32[512]{0:T(512)}, f32[2,512]{1,0:T(2,128)}, /*index=5*/s32[512]{0:T(512)}, s32[51...) while((s32[]{:T(128)}, f32[80,2048]{1,0:T(8,128)S(1)}, ...), condition=%wide.region_1.2_spmd.clone, body=%wide.region_0.1_spmd.clone.sunk | while | flops 88472600 | bytes 1523085 | solution.py:148
  16.9 62.5 %fusion.121 = f32[2048,2048,1]{1,0,2:T(8,128)} fusion(s32[2048]{0:T(1024)S(1)} %multiply_add_fusion, f32[2048]{0:T(1024)S(1)} %fusion.66), kind=kLoop, calls=%fused_computation.64.clone.1 | loop fusion | flops 62914560 | bytes 16793600 | tf_op jit(solution)/shard_map/dot_general | solution.py:84
  84.1 62.5 %fusion.44.clone.4 = f32[2048,2048,1]{1,0,2:T(8,128)} fusion(s32[2048]{0:T(1024)S(1)} %multiply_add_fusion, f32[2048]{0:T(1024)S(1)} %fusion.66), kind=kLoop, calls=%fused_computation.62.clone.clone.clone.1 | loop fusion | flops 62914560 | bytes 16793600 | tf_op jit(solution)/shard_map/reduce_sum | solution.py:191
  148.0 18.5 %fusion.45 = f32[4,8,2048]{2,1,0:T(8,128)S(1)} fusion(f32[4,8,2048]{2,1,0:T(8,128)S(1)} %get-tuple-element.415, f32[2048,2048,1]{1,0,2:T(8,128)} %fusion.121), kind=kOutput, calls=%fused_computation.63 | convolution fusion | flops 1610612736 | bytes 17301504 | tf_op jit(solution)/shard_map/dot_general | solution.py:84
  176.8 13.2 %all-to-all-start.1 = ((f32[128,1,512]{2,1,0:T(1,128)}), f32[128,1,512]{2,1,0:T(1,128)S(1)}, u32[]{:S(2)}, u32[]{:S(2)}) async-start(f32[128,1,512]{2,1,0:T(1,128)} %reshape.410), calls=%async_computation.1 | async-start | bytes 524288 | tf_op jit(solution)/shard_map/all_to_all | solution.py:163
  190.1 14.7 %all-to-all-done.1 = f32[128,1,512]{2,1,0:T(1,128)S(1)} async-done(((f32[128,1,512]{2,1,0:T(1,128)}), f32[128,1,512]{2,1,0:T(1,128)S(1)}, u32[]{:S(2)}, u32[]{:S(2)}) %all-to-all-start.1) | async-done | bytes 262176 | tf_op jit(solution)/shard_map/all_to_all | solution.py:163
  229.4 7.5 %copy.67 = f32[4,128,2,8,8]{3,2,1,4,0:T(2,128)} copy(f32[4,128,2,8,8]{3,1,4,2,0:T(8,128)} %bitcast.140) | data formatting | bytes 524288 | tf_op jit(solution)/shard_map/transpose | solution.py:99
  236.9 7.9 %reshape.392 = f32[4,2048,8]{1,2,0:T(8,128)S(1)} reshape(f32[4,128,2,8,8]{3,2,1,4,0:T(2,128)} %copy.67) | data formatting | bytes 524288 | tf_op jit(solution)/shard_map/reshape | solution.py:99
  244.8 19.3 %multiply_reduce_fusion.1 = (f32[]{:T(128)}, f32[4,8,2048]{2,1,0:T(8,128)S(1)}) fusion(f32[8,2048]{1,0:T(8,128)S(1)} %select_multiply_fusion, pred[8,2048]{1,0:T(8,128)(4,1)S(1)} %add_compare_fusion, f32[4,2048,8]{1,2,0:T(8,128)S(1)} %reshape.392, f32[2048,2048,1]{1,0,2:T(8,128)} %fusion.44.clone.4), kind=kOutput, calls=%fused_computation.85 | convolution fusion | flops 1610874880 | bytes 17383428 | tf_op jit(solution)/shard_map/dot_general | solution.py:84
  264.1 72.3 %fusion.41 = f32[4,8,2048]{2,1,0:T(8,128)S(1)} fusion(s32[2048]{0:T(1024)S(1)} %multiply_add_fusion, f32[2048]{0:T(1024)S(1)} %fusion.66, f32[8]{0:T(128)S(1)} %get-tuple-element.487, f32[4,8,2048]{2,1,0:T(8,128)S(1)} %get-tuple-element.486, f32[8,2048]{1,0:T(8,128)S(1)} %select_multiply_fusion, pred[8,2048]{1,0:T(8,128)(4,1)S(1)} %add_compare_fusion), kind=kOutput, calls=%fused_computation.59 | convolution fusion | flops 1673723904 | bytes 622624 | tf_op jit(solution)/shard_map/dot_general | solution.py:84
  347.3 8.2 %all-to-all-start.3 = ((f32[256,1,256]{2,1,0:T(1,128)}), f32[256,1,256]{2,1,0:T(1,128)S(1)}, u32[]{:S(2)}, u32[]{:S(2)}) async-start(f32[256,1,256]{2,1,0:T(1,128)} %reshape.412), calls=%async_computation.3 | async-start | bytes 524288 | tf_op jit(solution)/shard_map/all_to_all | solution.py:45
  355.4 72.9 %fusion.35 = f32[4,8,2048]{2,1,0:T(8,128)S(1)} fusion(s32[2048]{0:T(1024)S(1)} %multiply_add_fusion, f32[2048]{0:T(1024)S(1)} %fusion.66, f32[2048]{0:T(1024)S(1)} %convert_multiply_fusion, f32[4,8,2048]{2,1,0:T(8,128)S(1)} %get-tuple-element.486, f32[8,2048]{1,0:T(8,128)S(1)} %select_multiply_fusion, pred[8,2048]{1,0:T(8,128)(4,1)S(1)} %add_compare_fusion), kind=kOutput, calls=%fused_computation.53 | convolution fusion | flops 1673723904 | bytes 630784 | tf_op jit(solution)/shard_map/dot_general | solution.py:84
  439.2 13.9 %all-to-all-start.4 = ((f32[256,1,256]{2,1,0:T(1,128)}), f32[256,1,256]{2,1,0:T(1,128)S(1)}, u32[]{:S(2)}, u32[]{:S(2)}) async-start(f32[256,1,256]{2,1,0:T(1,128)} %reshape.414), calls=%async_computation.4 | async-start | bytes 524288 | tf_op jit(solution)/shard_map/all_to_all | solution.py:45
  471.2 7.5 %copy.71 = f32[4,128,2,8,8]{3,2,1,4,0:T(2,128)} copy(f32[4,128,2,8,8]{3,1,4,2,0:T(8,128)} %bitcast.145) | data formatting | bytes 524288 | tf_op jit(solution)/shard_map/transpose | solution.py:99
  478.7 7.9 %reshape.397 = f32[4,2048,8]{1,2,0:T(8,128)S(1)} reshape(f32[4,128,2,8,8]{3,2,1,4,0:T(2,128)} %copy.71) | data formatting | bytes 524288 | tf_op jit(solution)/shard_map/reshape | solution.py:99
  486.6 73.5 %fusion.96 = (bf16[4,8,2048]{2,1,0:T(8,128)(2,1)S(1)}, f32[4,8,2048]{2,1,0:T(8,128)}) fusion(f32[4,2048,8]{1,2,0:T(8,128)S(1)} %reshape.397, s32[2048]{0:T(1024)S(1)} %multiply_add_fusion, f32[2048]{0:T(1024)S(1)} %fusion.66), kind=kOutput, calls=%fused_computation.132 | convolution fusion | flops 1673592832 | bytes 671744 | tf_op jit(solution)/shard_map/dot_general | solution.py:84
  578.3 7.5 %copy.75 = f32[4,128,2,8,8]{3,2,1,4,0:T(2,128)} copy(f32[4,128,2,8,8]{3,1,4,2,0:T(8,128)} %bitcast.148) | data formatting | bytes 524288 | tf_op jit(solution)/shard_map/transpose | solution.py:99
  585.8 7.9 %reshape.402 = f32[4,2048,8]{1,2,0:T(8,128)S(1)} reshape(f32[4,128,2,8,8]{3,2,1,4,0:T(2,128)} %copy.75) | data formatting | bytes 524288 | tf_op jit(solution)/shard_map/reshape | solution.py:99
  593.7 72.6 %fusion.95 = (bf16[4,8,2048]{2,1,0:T(8,128)(2,1)S(1)}, f32[4,8,2048]{2,1,0:T(8,128)}) fusion(f32[4,2048,8]{1,2,0:T(8,128)S(1)} %reshape.402, s32[2048]{0:T(1024)S(1)} %multiply_add_fusion, f32[2048]{0:T(1024)S(1)} %fusion.66), kind=kOutput, calls=%fused_computation.131 | convolution fusion | flops 1673592832 | bytes 671744 | tf_op jit(solution)/shard_map/dot_general | solution.py:84
  666.5 8.6 %all_to_all.53 = bf16[2,8,8,2048]{3,2,1,0:T(8,128)(2,1)S(1)} all-to-all(bf16[2,8,8,2048]{3,2,1,0:T(8,128)(2,1)S(1)} %broadcast_in_dim.108), channel_id=1, replica_groups=mesh['slab_0'=4,'slab_1'=4,'slab_2'=4,'slab_3'=2,'cell'=2] {'cell'}, dimensions={0} | all-to-all | bytes 1048576 | tf_op jit(solution)/shard_map/all_to_all | solution.py:52
  681.3 9.2 %all-reduce.2 = (f32[]{:T(128)}, f32[]{:T(128)}, f32[]{:T(128)}) all-reduce(f32[]{:T(128)S(6)} %div.16, f32[]{:T(128)} %maximum_reduce_fusion, f32[]{:T(128)} %get-tuple-element.414), channel_id=1, replica_groups=mesh['slab_0'=4,'slab_1'=4,'slab_2'=4,'slab_3'=2,'cell'=2] {'slab_0'}, use_global_device_ids=true, to_apply=%region_7.8 | all-reduce | flops 3 | bytes 24 | tf_op jit(solution)/shard_map/psum | solution.py:61
  690.6 9.3 %all-reduce.1 = (f32[]{:T(128)}, f32[]{:T(128)}, f32[]{:T(128)}) all-reduce(f32[]{:T(128)} %get-tuple-element.460, f32[]{:T(128)} %get-tuple-element.461, f32[]{:T(128)} %get-tuple-element.462), channel_id=1, replica_groups=mesh['slab_0'=4,'slab_1'=4,'slab_2'=4,'slab_3'=2,'cell'=2] {'slab_1'}, use_global_device_ids=true, to_apply=%region_8.9 | all-reduce | flops 3 | bytes 24 | tf_op jit(solution)/shard_map/psum | solution.py:61
  699.9 12.1 %all-reduce = (f32[]{:T(128)}, f32[]{:T(128)}, f32[]{:T(128)}) all-reduce(f32[]{:T(128)} %get-tuple-element.457, f32[]{:T(128)} %get-tuple-element.458, f32[]{:T(128)} %get-tuple-element.459), channel_id=1, replica_groups=mesh['slab_0'=4,'slab_1'=4,'slab_2'=4,'slab_3'=2,'cell'=2] {'slab_2'}, use_global_device_ids=true, to_apply=%region_9.10 | all-reduce | flops 3 | bytes 24 | tf_op jit(solution)/shard_map/psum | solution.py:61
  711.9 9.6 %all-reduce.4 = (f32[]{:T(128)}, f32[]{:T(128)}, f32[]{:T(128)}) all-reduce(f32[]{:T(128)} %get-tuple-element.454, f32[]{:T(128)} %get-tuple-element.455, f32[]{:T(128)} %get-tuple-element.456), channel_id=1, replica_groups=mesh['slab_0'=4,'slab_1'=4,'slab_2'=4,'slab_3'=2,'cell'=2] {'slab_3'}, use_global_device_ids=true, to_apply=%region_10.11 | all-reduce | flops 3 | bytes 24 | tf_op jit(solution)/shard_map/psum | solution.py:61
  (132 shorter events, 131.5 us)
Async XLA Ops:
  10.6 68.9 %collective-permute-start = (bf16[4,4,2048]{2,1,0:T(4,128)(2,1)S(1)}, bf16[4,4,2048]{2,1,0:T(4,128)(2,1)S(1)}, u32[]{:S(2)}, u32[]{:S(2)}) collective-permute-start(bf16[4,4,2048]{2,1,0:T(4,128)(2,1)S(1)} %slice.75), channel_id=1, source_target_pairs={{0,2},{2,4},{4,6},{6,8},{8,10},{10,12},{12,14},{14,16},{16,18},{18... | collective-permute-start | bytes 196616 | tf_op jit(solution)/shard_map/ppermute | solution.py:19
  80.4 66.2 %all-to-all-start = ((f32[2,4,8,2048]{3,2,1,0:T(8,128)}), f32[2,4,8,2048]{3,2,1,0:T(8,128)S(1)}, u32[]{:S(2)}, u32[]{:S(2)}) async-start(f32[2,4,8,2048]{3,2,1,0:T(8,128)} %copy_bitcast_fusion.1), calls=%async_computation | async-start | bytes 1048576 | tf_op jit(solution)/shard_map/all_to_all | solution.py:29
  147.3 0.7 copy-start
  176.8 28.1 %all-to-all-start.1 = ((f32[128,1,512]{2,1,0:T(1,128)}), f32[128,1,512]{2,1,0:T(1,128)S(1)}, u32[]{:S(2)}, u32[]{:S(2)}) async-start(f32[128,1,512]{2,1,0:T(1,128)} %reshape.410), calls=%async_computation.1 | async-start | bytes 524288 | tf_op jit(solution)/shard_map/all_to_all | solution.py:163
  217.7 7.5 %all-to-all-start.2 = ((f32[4,1024,16]{1,0,2:T(4,128)}), f32[4,1024,16]{1,0,2:T(4,128)S(1)}, u32[]{:S(2)}, u32[]{:S(2)}) async-start(f32[4,1024,16]{1,0,2:T(4,128)} %copy.65), calls=%async_computation.2 | async-start | bytes 524288 | tf_op jit(solution)/shard_map/all_to_all | solution.py:162
  347.3 91.9 %all-to-all-start.3 = ((f32[256,1,256]{2,1,0:T(1,128)}), f32[256,1,256]{2,1,0:T(1,128)S(1)}, u32[]{:S(2)}, u32[]{:S(2)}) async-start(f32[256,1,256]{2,1,0:T(1,128)} %reshape.412), calls=%async_computation.3 | async-start | bytes 524288 | tf_op jit(solution)/shard_map/all_to_all | solution.py:45
  439.2 120.9 %all-to-all-start.4 = ((f32[256,1,256]{2,1,0:T(1,128)}), f32[256,1,256]{2,1,0:T(1,128)S(1)}, u32[]{:S(2)}, u32[]{:S(2)}) async-start(f32[256,1,256]{2,1,0:T(1,128)} %reshape.414), calls=%async_computation.4 | async-start | bytes 524288 | tf_op jit(solution)/shard_map/all_to_all | solution.py:45
  593.7 86.3 %copy-start.1 = (f32[4,8,2048]{2,1,0:T(8,128)S(1)}, f32[4,8,2048]{2,1,0:T(8,128)}, u32[]{:S(2)}) copy-start(f32[4,8,2048]{2,1,0:T(8,128)} %copy-done) | copy-start | bytes 786436
  593.7 133.8 %copy-start.2 = (f32[2,512]{1,0:T(2,128)S(1)}, f32[2,512]{1,0:T(2,128)}, u32[]{:S(2)}) copy-start(f32[2,512]{1,0:T(2,128)} %get-tuple-element.715) | copy-start | bytes 12292
  593.7 133.8 %copy-start.3 = (s32[512]{0:T(512)S(1)}, s32[512]{0:T(512)}, u32[]{:S(2)}) copy-start(s32[512]{0:T(512)} %get-tuple-element.718) | copy-start | bytes 6148
  593.7 133.8 %copy-start.4 = (s32[512]{0:T(512)S(1)}, s32[512]{0:T(512)}, u32[]{:S(2)}) copy-start(s32[512]{0:T(512)} %get-tuple-element.719) | copy-start | bytes 6148
  593.7 133.8 %copy-start.5 = (s32[512]{0:T(512)S(1)}, s32[512]{0:T(512)}, u32[]{:S(2)}) copy-start(s32[512]{0:T(512)} %get-tuple-element.720) | copy-start | bytes 6148
  593.7 133.8 %copy-start.6 = (s32[512]{0:T(512)S(1)}, s32[512]{0:T(512)}, u32[]{:S(2)}) copy-start(s32[512]{0:T(512)} %get-tuple-element.721) | copy-start | bytes 6148
  593.7 133.8 %copy-start.7 = (s32[512]{0:T(512)S(1)}, s32[512]{0:T(512)}, u32[]{:S(2)}) copy-start(s32[512]{0:T(512)} %get-tuple-element.722) | copy-start | bytes 6148
  675.2 52.0 %collective-permute-start.1 = (bf16[8,4,2048]{2,1,0:T(4,128)(2,1)S(1)}, bf16[8,4,2048]{2,1,0:T(4,128)(2,1)S(1)}, u32[]{:S(2)}, u32[]{:S(2)}) collective-permute-start(bf16[8,4,2048]{2,1,0:T(4,128)(2,1)S(1)} %slice.72), channel_id=1, source_target_pairs={{2,0},{4,2},{6,4},{8,6},{10,8},{12,10},{14,12},{16,14},{18,16},{20... | collective-permute-start | bytes 393224 | tf_op jit(solution)/shard_map/ppermute | solution.py:19
  730.4 0.6 copy-start.8
where the time goes:
time: 738 us; the launch traced here: 732 us
  matrix products  333 us (45%)
  other arithmetic  135 us (18%)
  local copies, waits for them, and re-layouts  135 us (18%)
  starting transfers between devices  53.4 us (7%)
  blocking collectives  53.2 us (7%)
  waiting for transfers between devices  18.7 us (3%)
    dot_general x6, matrix products, transform(): lax.dot_general(source, table, (((contract,), (table_dim,)), ((), ())), p...  329 us
    dot_general x1, other arithmetic, transform(): lax.dot_general(source, table, (((contract,), (table_dim,)), ((), ())), p...  62.5 us
    reduce_sum x1, other arithmetic, body(): energy_local = jnp.sum(spectrum * potential_hat) / (length * length)  62.5 us
    psum x5, blocking collectives, one_axis_at_a_time(): shard = lax.psum(shard, axis)  44.6 us
    unnamed x24, local copies, waits for them, and re-layouts  30.9 us
    reshape x3, local copies, waits for them, and re-layouts, natural_order(): return jnp.swapaxes(shaped, 1, 2).reshape(lead, total_len, tail)  23.6 us
    transpose x3, local copies, waits for them, and re-layouts, natural_order(): return jnp.swapaxes(shaped, 1, 2).reshape(lead, total_len, tail)  22.5 us
    all_to_all x2, starting transfers between devices, one_exchange(): lax.all_to_all(pieces, axis, split_axis=0, concat_axis=0, tiled=True)  22 us
  transfers between devices with their start and end apart: 7, of which 2 were waited for; matrix products, arithmetic and copies ran while one was open for 43% of the time, Pallas kernels for 0%

commit v1 on v0

v1 whole, which is shorter than its diff:
```python
import functools
import math

import jax
import jax.numpy as jnp
import numpy as np
from jax import lax
from jax.experimental import pallas as pl
from jax.experimental.pallas import tpu as pltpu
from jax.sharding import PartitionSpec as P

M = 2048
REGIONS = 4
SLABS = 128
CELLS_DEV = 512
BF = jnp.bfloat16
F32 = jnp.float32
MESH = pl.DeviceIdType.MESH
STEP = math.pi / M
R2 = math.sqrt(0.5)


def split_np(table):
    high = table.astype(np.float32).astype(BF)
    low = (table - high.astype(np.float64)).astype(np.float32).astype(BF)
    return np.stack([high, low])


def lanes_of(per_group, width):
    return np.repeat(per_group, width, axis=-1)


@functools.lru_cache(None)
def tables():
    pi = np.pi
    k2 = np.arange(64)[:, None]
    b = np.arange(128)[None, :]
    c1, s1 = np.cos(pi * k2 * (2 * b + 1) / 128), np.sin(pi * k2 * (2 * b + 1) / 128)
    c2, s2 = np.cos(pi * (k2 + 1) * (2 * b + 1) / 128), np.sin(pi * (k2 + 1) * (2 * b + 1) / 128)
    cm, sm = np.cos(pi * (2 * k2 + 1) * (2 * b + 1) / 256), np.sin(pi * (2 * k2 + 1) * (2 * b + 1) / 256)
    zero = np.zeros_like(c1)
    wc = np.block([[c1, s1], [c2, -s2]])
    wc0 = np.block([[c1, zero], [zero, cm]])
    ws = np.block([[s1, -c1], [s2, c2]])
    ws0 = np.block([[s1, zero], [zero, sm]])
    w_fwd = np.stack([split_np(wc), split_np(wc0)])
    w_inv = np.stack([split_np(w.T) for w in (ws, ws0, wc, wc0)]).reshape(2, 2, 2, 256, 128)
    kap = np.arange(16)
    ang = pi * kap[None, :] * (2 * np.arange(128)[:, None] + 1) / 4096
    tx = np.stack([lanes_of(np.cos(ang), 32), lanes_of(np.sin(ang), 32)]).astype(np.float32)
    a = np.arange(16)[:, None]
    j = np.arange(4)[None, :]
    wa = np.concatenate([np.cos(2 * pi * a * j / 32), np.sin(2 * pi * a * j / 32)])
    wa = lanes_of(wa, 32).astype(np.float32)
    p1 = np.arange(256)[:, None]
    d = np.arange(256)[None, :]
    cre, cim = np.cos(2 * pi * p1 * d / 512), -np.sin(2 * pi * p1 * d / 512)
    cim[0] = (-1.0) ** np.arange(256)
    cy = np.concatenate([cre, cim], 0)
    cy_fwd, cy_inv = split_np(cy), split_np(cy.T)
    r = np.arange(8)
    angy = pi * p1 * (2 * r[None, :] + 1) / 4096
    ty = np.stack([np.tile(np.cos(angy), (1, 16)), np.tile(np.sin(angy), (1, 16))]).astype(np.float32)
    p2 = np.arange(4)[None, :]
    rr = r[:, None]
    e0, e1 = pi * p2 * (2 * rr + 1) / 8, pi * (p2 + 1) * (2 * rr + 1) / 8
    em = pi * (2 * rr + 1) * (1 + 2 * p2) / 16
    z8 = np.zeros((8, 4))
    bc = (np.block([np.cos(e0), np.cos(e1)]), np.block([np.sin(e0), -np.sin(e1)]))
    bc0 = (np.block([np.cos(e0), z8]), np.block([z8, np.cos(em)]))
    bs = (np.block([np.sin(e0), np.sin(e1)]), np.block([-np.cos(e0), np.cos(e1)]))
    bs0 = (np.block([np.sin(e0), z8]), np.block([z8, np.sin(em)]))

    def wide(pair):
        return np.concatenate([np.kron(np.eye(16), part) for part in pair], 0)

    b_fwd = np.stack([split_np(wide(bc)), split_np(wide(bc0))])
    b_inv = np.stack([split_np(wide(m).T) for m in (bc, bc0, bs, bs0)]).reshape(2, 2, 2, 128, 256)
    join = np.tile(np.eye(32), (1, 4)).astype(np.float32).astype(BF)
    return w_fwd, w_inv, tx, wa, cy_fwd, cy_inv, ty, b_fwd, b_inv, join


def dot(x, y):
    return lax.dot_general(x, y, (((1,), (0,)), ((), ())), preferred_element_type=F32)


def dot_nt(x, y):
    return lax.dot_general(x, y, (((1,), (1,)), ((), ())), preferred_element_type=F32)


def split(x):
    high = x.astype(BF)
    return high, (x - high.astype(F32)).astype(BF)


def dot3(x, y):
    return dot(x[0], y[0]) + (dot(x[0], y[1]) + dot(x[1], y[0]))


def place():
    slab = lax.axis_index("slab")
    cell = lax.axis_index("cell")
    return slab, cell, lax.div(slab, 8), lax.rem(slab, 8) * 2 + cell


def device_at(plane, column):
    return (plane * 8 + lax.div(column, 2), lax.rem(column, 2))


def overlap(bins, low, high):
    return jnp.maximum(jnp.minimum(bins + 1.0, high) - jnp.maximum(bins, low), 0.0)


def kernel(
    cellp, w_fwd, w_inv, tx, wa, cy_fwd, cy_inv, ty, b_fwd, b_inv, join,
    field_x, field_y, force, sums,
    cb, xb, yr, d4, zs, s1, r1, us, vs, gs, s2, r2, ps, fb, pf, pr, e1, e2, es,
    col_sem, cell_s, cell_r, a1_s, a1_r, a2_s, a2_r, f_s, f_r, e_s, e_r,
):
    slab, cell, plane, column = place()
    me = plane * 16 + column
    has_prev = jnp.logical_and(cell == 0, slab > 0)
    barrier = pltpu.get_barrier_semaphore()

    def signal_at(sem, device):
        pl.semaphore_signal(sem, inc=1, device_id=device, device_id_type=MESH)

    for i in range(1, 16):
        signal_at(barrier, device_at(lax.rem(plane + i, 16), column))
        signal_at(barrier, device_at(plane, lax.rem(column + i, 16)))

    @pl.when(has_prev)
    def _():
        signal_at(barrier, (slab - 1, 0))
        signal_at(barrier, (slab - 1, 1))

    cb[cell] = cellp[...]

    def make_cells(slot):
        values = cb[slot]

        def rows(i, carry):
            base = i * 128
            bins = (lax.broadcasted_iota(jnp.int32, (128, 128), 0) + base).astype(F32)
            for block in range(4):
                part = values[:, block * 128 : block * 128 + 128]
                got = overlap(bins - part[0:1], part[1:2], part[2:3])
                xb[slot, pl.ds(pl.multiple_of(base, 128), 128), block * 128 : block * 128 + 128] = got.astype(BF)
            return carry

        lax.fori_loop(0, 16, rows, 0)
        low_row = slab * 16 + cell * 8
        bins = (lax.broadcasted_iota(jnp.int32, (8, CELLS_DEV), 0) + low_row).astype(F32)
        got = overlap(bins - values[3:4], values[4:5], values[5:6])
        for g in range(REGIONS):
            yr[slot, 8 * g : 8 * g + 8, :] = jnp.where(values[6:7] == float(g), got, 0.0)

    def add_density(slot, fresh):
        rows = yr[slot].astype(BF)
        rows = jnp.concatenate([rows] * 4, axis=0)
        for i in range(4):
            at = slice(512 * i, 512 * i + 512)
            got = dot_nt(xb[slot, at, :], rows)
            if fresh:
                d4[at, :] = got
            else:
                d4[at, :] += got

    mine, other = cell, 1 - cell
    make_cells(mine)
    has_next = slab < SLABS - 1
    pl.semaphore_wait(barrier, 30 + has_next.astype(jnp.int32))
    for i in range(1, 16):
        signal_at(col_sem, device_at(plane, lax.rem(column + i, 16)))

    def send(src, dst, s_sem, r_sem, device):
        return pltpu.make_async_remote_copy(
            src_ref=src, dst_ref=dst, send_sem=s_sem, recv_sem=r_sem, device_id=device, device_id_type=MESH
        )

    to_partner = send(cellp, cb.at[cell], cell_s.at[0], cell_r.at[cell], (slab, other))
    to_next = send(cellp, cb.at[2 + cell], cell_s.at[1], cell_r.at[2 + cell], (slab + 1, 0))
    to_partner.start()

    @pl.when(has_next)
    def _():
        to_next.start()

    add_density(mine, True)
    send(cellp, cb.at[other], cell_s.at[0], cell_r.at[other], (slab, other)).wait_recv()
    make_cells(other)
    add_density(other, False)

    @pl.when(has_prev)
    def _():
        for k in range(2):
            send(cellp, cb.at[2 + k], cell_s.at[0], cell_r.at[2 + k], (slab, other)).wait_recv()
            make_cells(2 + k)
            add_density(2 + k, False)

    def tally(i, carry):
        excess, area = carry
        got = d4[pl.ds(pl.multiple_of(i * 64, 64), 64), :].reshape(8, 8, 128)
        return excess + jnp.sum(jnp.maximum(got - 1.0, 0.0), axis=0), area + jnp.sum(got, axis=0)

    zero8 = jnp.zeros((8, 128), F32)
    excess, area = lax.fori_loop(0, 32, tally, (zero8, zero8))

    lane = lax.broadcasted_iota(jnp.int32, (1, 128), 1)
    first_group = lane < 32
    group_mask = first_group.astype(F32)

    def x_chunk(i, carry):
        at = pl.multiple_of(i * 16, 16)
        d = [d4[pl.ds(pl.multiple_of(128 * a + at, 16), 16), :] for a in range(16)]
        er = [d[m] * wa[m : m + 1, :] + d[m + 8] * wa[m + 8 : m + 9, :] for m in range(8)]
        ei = [-(d[m] * wa[16 + m : 17 + m, :] + d[m + 8] * wa[24 + m : 25 + m, :]) for m in range(8)]
        sr = [er[m] + er[m + 4] for m in range(4)]
        si = [ei[m] + ei[m + 4] for m in range(4)]
        tr = [er[m] - er[m + 4] for m in range(4)]
        ti = [ei[m] - ei[m + 4] for m in range(4)]
        ur = [tr[0], (tr[1] + ti[1]) * R2, ti[2], (ti[3] - tr[3]) * R2]
        ui = [ti[0], (ti[1] - tr[1]) * R2, -tr[2], -(tr[3] + ti[3]) * R2]

        def ends(re, im):
            ar, ai, br, bi = re[0] + re[2], im[0] + im[2], re[1] + re[3], im[1] + im[3]
            cr, ci, dr, di = re[0] - re[2], im[0] - im[2], re[1] - re[3], im[1] - im[3]
            return (ar + br, ai + bi), (cr + di, ci - dr), ar - br

        y0, y2, alternate = ends(sr, si)
        y1, y3, _ = ends(ur, ui)
        y0 = (y0[0], y0[1] + alternate * group_mask)
        for t, (re, im) in enumerate((y0, y1, y2, y3)):
            lanes = slice(128 * t, 128 * t + 128)
            c, s = tx[0, pl.ds(at, 16), lanes], tx[1, pl.ds(at, 16), lanes]
            for half, value in enumerate((re * c + im * s, im * c - re * s)):
                high, low = split(value)
                zs[0, pl.ds(half * 128 + at, 16), lanes] = high
                zs[1, pl.ds(half * 128 + at, 16), lanes] = low
        return carry

    lax.fori_loop(0, 8, x_chunk, 0)
    for t in range(4):
        lanes = slice(128 * t, 128 * t + 128)
        z = (zs[0, 0:256, lanes], zs[1, 0:256, lanes])
        got = dot3((w_fwd[0, 0], w_fwd[0, 1]), z)
        if t == 0:
            got = jnp.where(first_group, dot3((w_fwd[1, 0], w_fwd[1, 1]), z), got)
        s1[t // 2, 128 * (t % 2) : 128 * (t % 2) + 128, :] = got

    pl.semaphore_wait(col_sem, 15)

    def exchange(src, dst, s_sem, r_sem):
        def to(i, k):
            there, across = lax.rem(plane + i, 16), lax.rem(column + k, 16)
            send(
                src.at[:, there * 16 + across], dst.at[:, me], s_sem, r_sem, device_at(there, across)
            ).start()

        def planes(i, carry):
            for k in range(16):
                to(i, k)
            return carry

        lax.fori_loop(1, 16, planes, 0)
        for k in range(1, 16):
            to(0, k)
        dst[:, pl.ds(me, 1), :] = src[:, pl.ds(me, 1), :]

    def exchange_wait(src, dst, s_sem, r_sem):
        whole = send(src.at[:, pl.ds(0, 255)], dst.at[:, pl.ds(0, 255)], s_sem, r_sem, (slab, other))
        whole.wait_recv()
        whole.wait_send()

    exchange(s1, r1, a1_s, a1_r)
    exchange_wait(s1, r1, a1_s, a1_r)

    high, low = zip(*(split(r1[h]) for h in range(2)))
    whole = (jnp.concatenate(high, axis=1), jnp.concatenate(low, axis=1))
    us[...] = dot3((cy_fwd[0], cy_fwd[1]), whole)

    def y_chunk(i, carry):
        at = pl.multiple_of(i * 16, 16)
        c, s = ty[0, pl.ds(at, 16), :], ty[1, pl.ds(at, 16), :]
        for h in range(2):
            lanes = slice(128 * h, 128 * h + 128)
            re, im = us[pl.ds(at, 16), lanes], us[pl.ds(256 + at, 16), lanes]
            for half, value in enumerate((re * c + im * s, im * c - re * s)):
                parts = split(value)
                for k in range(2):
                    vs[k, pl.ds(256 * h + at, 16), 128 * half : 128 * half + 128] = parts[k]
        return carry

    lax.fori_loop(0, 16, y_chunk, 0)
    gs[...] = dot3((vs[0, 0:512], vs[1, 0:512]), (b_fwd[0, 0], b_fwd[0, 1]))
    top_row = lax.broadcasted_iota(jnp.int32, (16, 1), 0) == 0
    for h in range(2):
        at = slice(256 * h, 256 * h + 16)
        fixed = dot3((vs[0, at], vs[1, at]), (b_fwd[1, 0], b_fwd[1, 1]))
        gs[at, :] = jnp.where(top_row, fixed, gs[at, :])

    tile, k2c = lax.div(me, 128), lax.rem(me, 128)
    lower = k2c < 64
    group = lax.div(lane, 32)
    order = lax.rem(lane, 8)
    energy = zero8
    for h in range(2):
        kap = 4 * (tile + 2 * h) + group
        q = jnp.where(
            kap == 0,
            jnp.where(lower, 32 * k2c, 16 + 32 * (k2c - 64)),
            jnp.where(lower, kap + 32 * k2c, 32 - kap + 32 * (k2c - 64)),
        )
        qf = q.astype(F32)
        aq = jnp.where(q == 0, 1.0 / M, 2.0 / M)

        def scale(i, energy, h=h, qf=qf, aq=aq):
            at = pl.multiple_of(i * 16, 16)
            p1 = lax.broadcasted_iota(jnp.int32, (16, 128), 0) + at
            up = order < 4
            p = jnp.where(up, p1 + 512 * order, 512 - p1 + 512 * (order - 4))
            p = jnp.where(jnp.logical_and(p1 == 0, jnp.logical_not(up)), 256 + 512 * (order - 4), p)
            pf_ = p.astype(F32)
            k2 = pf_ * pf_ + qf * qf
            inverse = jnp.where(k2 == 0.0, 0.0, 1.0 / jnp.where(k2 == 0.0, 1.0, k2))
            value = gs[pl.ds(256 * h + at, 16), :]
            weighted = value * (jnp.where(p == 0, 1.0 / M, 2.0 / M) * aq * inverse)
            work = weighted * value
            base = weighted * (1.0 / STEP)
            for f, part in enumerate((base * qf, base * pf_)):
                parts = split(part)
                for k in range(2):
                    vs[k, pl.ds(512 * f + 256 * h + at, 16), 0:128] = parts[k]
            return energy + (work[0:8] + work[8:16])

        energy = lax.fori_loop(0, 16, scale, energy)

    for f in range(2):
        rows = slice(512 * f, 512 * f + 512)
        drive = (vs[0, rows, 0:128], vs[1, rows, 0:128])
        us[...] = dot3(drive, (b_inv[f, 0, 0], b_inv[f, 0, 1]))
        for h in range(2):
            at = slice(256 * h, 256 * h + 16)
            src = slice(512 * f + 256 * h, 512 * f + 256 * h + 16)
            fixed = dot3((vs[0, src, 0:128], vs[1, src, 0:128]), (b_inv[f, 1, 0], b_inv[f, 1, 1]))
            us[at, :] = jnp.where(top_row, fixed, us[at, :])

        def back_chunk(i, carry, f=f):
            at = pl.multiple_of(i * 16, 16)
            c, s = ty[0, pl.ds(at, 16), :], ty[1, pl.ds(at, 16), :]
            for h in range(2):
                re, im = us[pl.ds(256 * h + at, 16), 0:128], us[pl.ds(256 * h + at, 16), 128:256]
                lanes = slice(256 * f + 128 * h, 256 * f + 128 * h + 128)
                for half, value in enumerate((re * c - im * s, re * s + im * c)):
                    parts = split(value)
                    for k in range(2):
                        zs[k, pl.ds(256 * half + at, 16), lanes] = parts[k]
            return carry

        lax.fori_loop(0, 16, back_chunk, 0)
    for t in range(4):
        lanes = slice(128 * t, 128 * t + 128)
        s2[t] = dot3((cy_inv[0], cy_inv[1]), (zs[0, :, lanes], zs[1, :, lanes]))

    exchange(s2, r2, a2_s, a2_r)

    def total(x):
        return jnp.sum(jnp.sum(x, axis=1, keepdims=True), axis=0, keepdims=True)

    row = jnp.where(lane == 0, total(excess) * 0.25, jnp.where(lane == 1, total(area) * 0.25, total(energy) * (1.0 / (STEP * STEP * M * M))))
    es[0] = row
    e1[plane] = row
    for i in range(1, 16):
        send(es.at[0], e1.at[plane], e_s.at[0], e_r.at[0], device_at(lax.rem(plane + i, 16), column)).start()
    exchange_wait(s2, r2, a2_s, a2_r)
    sums_wait = send(e1.at[pl.ds(0, 15)], e1.at[pl.ds(0, 15)], e_s.at[0], e_r.at[0], (slab, other))
    sums_wait.wait_recv()
    sums_wait.wait_send()
    row = jnp.sum(e1[...], axis=0)
    es[1] = row
    e2[column] = row
    for i in range(1, 16):
        send(es.at[1], e2.at[column], e_s.at[1], e_r.at[1], device_at(plane, lax.rem(column + i, 16))).start()

    for f, out in enumerate((field_x, field_y)):
        for t in range(4):
            lanes = slice(128 * t, 128 * t + 128)
            o = split(r2[2 * f + t // 2, 128 * (t % 2) : 128 * (t % 2) + 128, :])
            got = dot3((w_inv[f, 0, 0], w_inv[f, 0, 1]), o)
            if t == 0:
                got = jnp.where(first_group, dot3((w_inv[f, 1, 0], w_inv[f, 1, 1]), o), got)
            d4[512 * t : 512 * t + 256, :] = got

        def out_chunk(i, carry):
            at = pl.multiple_of(i * 16, 16)
            yr_, yi_ = [], []
            for t in range(4):
                lanes = slice(128 * t, 128 * t + 128)
                c, s = tx[0, pl.ds(at, 16), lanes], tx[1, pl.ds(at, 16), lanes]
                re, im = d4[pl.ds(512 * t + at, 16), :], d4[pl.ds(512 * t + 128 + at, 16), :]
                yr_.append(re * c - im * s)
                yi_.append(re * s + im * c)
            mid = yi_[0] * group_mask

            def four(re, im):
                ar, ai, br, bi = re[0] + re[2], im[0] + im[2], re[1] + re[3], im[1] + im[3]
                cr, ci, dr, di = re[0] - re[2], im[0] - im[2], re[1] - re[3], im[1] - im[3]
                return (ar + br, ai + bi), (cr - di, ci + dr), (ar - br, ai - bi), (cr + di, ci - dr)

            m0, m2, m4, m6 = four(yr_, yi_)
            ur = [yr_[0], (yr_[1] - yi_[1]) * R2, -yi_[2], -(yr_[3] + yi_[3]) * R2]
            ui = [yi_[0], (yr_[1] + yi_[1]) * R2, yr_[2], (yr_[3] - yi_[3]) * R2]
            m1, m3, m5, m7 = four(ur, ui)
            for m, (re, im) in enumerate((m0, m1, m2, m3, m4, m5, m6, m7)):
                re = re + mid if m % 2 == 0 else re - mid
                for a in (m, m + 8):
                    parts = split(re * wa[a : a + 1, :] - im * wa[16 + a : 17 + a, :])
                    for k in range(2):
                        ps[k, pl.ds(128 * a + at, 16), :] = parts[k]
            return carry

        lax.fori_loop(0, 8, out_chunk, 0)
        for i in range(8):
            at = slice(256 * i, 256 * i + 256)
            got = dot_nt(join[...], ps[0, at, :]) + dot_nt(join[...], ps[1, at, :])
            for g in range(REGIONS):
                out[g, :, at] = got[8 * g : 8 * g + 8, :]
            fb[32 * f : 32 * f + 32, at] = got.astype(BF)

    def push(slot):
        got = dot(fb[...], xb[slot])
        rows = yr[slot].astype(BF).astype(F32)
        for f in range(2):
            pf[slot, f : f + 1, :] = jnp.sum(got[32 * f : 32 * f + 32, :] * rows, axis=0, keepdims=True)

    def give_back(slot, device, sem, into):
        return send(pf.at[slot], pr.at[into], f_s.at[sem], f_r.at[into], device)

    push(other)
    give_back(other, (slab, other), 0, 0).start()

    @pl.when(has_prev)
    def _():
        for k in range(2):
            push(2 + k)
            give_back(2 + k, (slab - 1, k), 1 + k, 1).start()

    push(mine)
    pr[2] = jnp.zeros((2, CELLS_DEV), F32)
    give_back(other, (slab, other), 0, 0).wait_recv()

    @pl.when(has_next)
    def _():
        give_back(other, (slab, other), 0, 1).wait_recv()

    @pl.when(jnp.logical_not(has_next))
    def _():
        pr[1] = jnp.zeros((2, CELLS_DEV), F32)

    force[...] = pf[mine] + pr[0] + pr[1]

    send(e2.at[pl.ds(0, 15)], e2.at[pl.ds(0, 15)], e_s.at[1], e_r.at[1], (slab, other)).wait()
    sums[...] = jnp.broadcast_to(jnp.sum(e2[...], axis=0), (8, 128))

    give_back(other, (slab, other), 0, 0).wait_send()
    to_partner.wait_send()

    @pl.when(has_prev)
    def _():
        for k in range(2):
            give_back(2 + k, (slab - 1, k), 1 + k, 1).wait_send()

    @pl.when(has_next)
    def _():
        to_next.wait_send()


def body(cell_row, cell_col, cell_width, cell_height, cell_region, cell_offset):
    off = cell_offset
    cellp = jnp.stack(
        [
            cell_col.astype(F32),
            off[0],
            off[0] + cell_width.astype(F32),
            cell_row.astype(F32),
            off[1],
            off[1] + cell_height.astype(F32),
            cell_region.astype(F32),
            off[0],
        ]
    )
    consts = [jnp.asarray(t) for t in tables()]
    vmem = pl.BlockSpec(memory_space=pltpu.VMEM)
    V = pltpu.VMEM
    D = pltpu.SemaphoreType.DMA
    scratch = [
        V((4, 8, CELLS_DEV), F32),
        V((4, M, CELLS_DEV), BF),
        V((4, 32, CELLS_DEV), F32),
        V((M, 128), F32),
        V((2, 512, 512), BF),
        V((2, 256, 128), F32),
        V((2, 256, 128), F32),
        V((512, 256), F32),
        V((2, 1024, 256), BF),
        V((512, 128), F32),
        V((4, 256, 128), F32),
        V((4, 256, 128), F32),
        V((2, M, 128), BF),
        V((64, M), BF),
        V((4, 2, CELLS_DEV), F32),
        V((3, 2, CELLS_DEV), F32),
        V((16, 1, 128), F32),
        V((16, 1, 128), F32),
        V((2, 1, 128), F32),
        pltpu.SemaphoreType.REGULAR,
        D((2,)), D((4,)),
        D, D, D, D,
        D((3,)), D((2,)),
        D((2,)), D((2,)),
    ]
    field_x, field_y, force, sums = pl.pallas_call(
        kernel,
        out_shape=(
            jax.ShapeDtypeStruct((REGIONS, 8, M), F32),
            jax.ShapeDtypeStruct((REGIONS, 8, M), F32),
            jax.ShapeDtypeStruct((2, CELLS_DEV), F32),
            jax.ShapeDtypeStruct((8, 128), F32),
        ),
        in_specs=[vmem] * (1 + len(consts)),
        out_specs=(vmem,) * 4,
        scratch_shapes=scratch,
        compiler_params=pltpu.CompilerParams(
            collective_id=0, has_side_effects=True, vmem_limit_bytes=60 * 1024 * 1024
        ),
        name="placement",
    )(cellp, *consts)
    overflow = sums[0, 0] / sums[0, 1]
    return (field_x, field_y, force, sums[0, 2], overflow)


def solution(mesh):
    both = ("slab", "cell")
    placed = (P(both),) * 5 + (P(None, both),)
    return jax.shard_map(
        body,
        mesh=mesh,
        in_specs=placed,
        out_specs=(P(None, both, None), P(None, both, None), P(None, both), P(), P()),
        check_vma=False,
    )
```

time: 738 us -> 70.5 us (0.10)
  matrix products: 333 us -> 0 us
  other arithmetic: 135 us -> 0.02 us
  local copies, waits for them, and re-layouts: 135 us -> 9.2 us
  Pallas kernels: 0 us -> 57.8 us
  starting transfers between devices: 53.4 us -> 0 us
  blocking collectives: 53.2 us -> 0 us
  waiting for transfers between devices: 18.7 us -> 0 us
    dot_general x10 -> x0, matrix products: 333 us -> none  [the longest x6 329 us: transform(): lax.dot_general(source, table, (((contract,), (table_dim,)), ((), ())), p...]
    reduce_sum x5 -> x0, other arithmetic: 64 us -> none  [the longest x1 62.5 us: body(): energy_local = jnp.sum(spectrum * potential_hat) / (length * length)]
    dot_general x1 -> x0, other arithmetic: 62.5 us -> none  [transform(): lax.dot_general(source, table, (((contract,), (table_dim,)), ((), ())), p...]
    pallas_call x0 -> x1, Pallas kernels: none -> 57.8 us  [body(): pl.pallas_call(kernel, out_shape=(jax.ShapeDtypeStruct((REGIONS, 8, M), F...]
    reshape x12 -> x0, local copies, waits for them, and re-layouts: 48.5 us -> none  [the longest x3 23.6 us: natural_order(): return jnp.swapaxes(shaped, 1, 2).reshape(lead, total_len, tail)]
    psum x5 -> x0, blocking collectives: 44.6 us -> none  [one_axis_at_a_time(): shard = lax.psum(shard, axis)]
    all_to_all x5 -> x0, starting transfers between devices: 42.3 us -> none  [the longest x2 22 us: one_exchange(): lax.all_to_all(pieces, axis, split_axis=0, concat_axis=0, tiled=True)]
    unnamed x24 -> x17, local copies, waits for them, and re-layouts: 30.9 us -> 6.41 us
  transfers between devices with their start and end apart: 7 -> 0, of which waited for: 2 -> 0; matrix products, arithmetic and copies ran while one was open for 43% -> 0% of each run, Pallas kernels for 0% -> 0%
where the time goes in v1:
time: 70.5 us; the launch traced here: 70.1 us
  Pallas kernels  57.8 us (82%)
  local copies, waits for them, and re-layouts  9.2 us (13%)
  between operations  3.13 us (4%)
    pallas_call x1, Pallas kernels, body(): pl.pallas_call(kernel, out_shape=(jax.ShapeDtypeStruct((REGIONS, 8, M), F...  57.8 us
    unnamed x17, local copies, waits for them, and re-layouts  6.41 us

profile of v1, /device:TPU:1, one launch (start us, length us, event | category | flops | bytes accessed | tf_op | source)
XLA Modules:
  0.0 70.1 jit_solution(13365246905963158723)
XLA Ops:
  0.6 0.8 %fusion.1 = (f32[1,512]{1,0:T(1,128)S(1)}, f32[1,512]{1,0:T(1,128)S(1)}) fusion(f32[2,512]{1,0:T(2,128)} %param.21), kind=kLoop, calls=%fused_computation.3 | loop fusion | bytes 8192 | tf_op jit(solution)/shard_map/slice | solution.py:486
  1.4 0.0 copy-start.2
  1.4 0.7 copy-done.2
  2.1 0.0 copy-start.3
  2.1 0.7 copy-done.3
  2.8 0.0 copy-start.4
  2.8 0.7 copy-done.4
  3.4 0.0 copy-start.5
  3.5 0.7 copy-done.5
  4.1 0.0 copy-start.6
  4.1 0.7 copy-done.6
  4.8 0.6 stack.23.cellp
  5.5 57.8 %placement.1 = (f32[4,8,2048]{2,1,0:T(8,128)}, f32[4,8,2048]{2,1,0:T(8,128)}, f32[2,512]{1,0:T(2,128)}, f32[8,128]{1,0:T(8,128)}) custom-call(f32[8,512]{1,0:T(8,128)} %stack.23.cellp, bf16[2,2,128,256]{3,2,1,0:T(8,128)(2,1)} %constant.20.clone.w_fwd, bf16[2,2,2,256,128]{4,3,2,1,0:T(8,128)(2,1)} %constant.21.clone.w_inv, f32[2,128,512]{2,1,0:T(8,128)} %constant.22.clone.tx, ...), custom_call_target="tpu_custom_call" | custom-call | tf_op jit(solution)/shard_map/placement/pallas_call | solution.py:522
  63.3 1.4 %fusion = (f32[1,1]{1,0:T(1,128)}, f32[1,1]{1,0:T(1,128)}, f32[1,1]{1,0:T(1,128)}) fusion(f32[8,128]{1,0:T(8,128)} %get-tuple-element.12), kind=kLoop, calls=%fused_computation.2 | loop fusion | bytes 24 | tf_op jit(solution)/shard_map/slice | solution.py:538
  66.0 0.0 copy-start
  66.0 1.7 %copy.24 = f32[4,8,2048]{2,1,0:T(8,128)} copy(f32[4,8,2048]{2,1,0:T(8,128)} %get-tuple-element.23) | data formatting | bytes 524288
  67.7 0.0 copy-done
  67.7 0.0 copy-start.1
  67.7 0.7 %copy.25 = f32[4,8,2048]{2,1,0:T(8,128)} copy(f32[4,8,2048]{2,1,0:T(8,128)S(1)} %copy-done) | data formatting | bytes 524288
  68.4 0.0 copy-done.1
  68.4 0.6 copy.26
  (5 shorter events, 0.0 us)
Async XLA Ops:
  1.4 0.7 copy-start.2
  2.1 0.7 copy-start.3
  2.8 0.7 copy-start.4
  3.4 0.7 copy-start.5
  4.1 0.7 copy-start.6
  66.0 1.7 %copy-start = (f32[4,8,2048]{2,1,0:T(8,128)S(1)}, f32[4,8,2048]{2,1,0:T(8,128)}, u32[]{:S(2)}) copy-start(f32[4,8,2048]{2,1,0:T(8,128)} %get-tuple-element.24) | copy-start | bytes 786436
  67.7 0.7 %copy-start.1 = (f32[2,512]{1,0:T(2,128)S(1)}, f32[2,512]{1,0:T(2,128)}, u32[]{:S(2)}) copy-start(f32[2,512]{1,0:T(2,128)} %get-tuple-element.25) | copy-start | bytes 12292

commit v2 on v1

v2 whole, which is shorter than its diff:
```python
import functools
import math

import jax
import jax.numpy as jnp
import numpy as np
from jax import lax
from jax.experimental import pallas as pl
from jax.experimental.pallas import tpu as pltpu
from jax.sharding import PartitionSpec as P

M = 2048
REGIONS = 4
SLABS = 128
CELLS_DEV = 512
BF = jnp.bfloat16
F32 = jnp.float32
I32 = jnp.int32
MESH = pl.DeviceIdType.MESH
STEP = math.pi / M


def c_add(x,y): return (x[0]+y[0], x[1]+y[1])
def c_sub(x,y): return (x[0]-y[0], x[1]-y[1])
def c_turn(x,angle):
    c,s=math.cos(angle),math.sin(angle)
    if abs(s)<1e-12: return x if c>0 else (-x[0],-x[1])
    if abs(c)<1e-12: return (-x[1],x[0]) if s>0 else (x[1],-x[0])
    if abs(abs(c)-abs(s))<1e-12:
        h=abs(c); a,b=x[0],x[1]
        sc,ss=(1 if c>0 else -1),(1 if s>0 else -1)
        def lin(p,a,q,b):
            if p>0: return (a+b)*h if q>0 else (a-b)*h
            return (b-a)*h if q>0 else (a+b)*(-h)
        return (lin(sc,a,-ss,b), lin(ss,a,sc,b))
    return (x[0]*c-x[1]*s, x[0]*s+x[1]*c)
def c_fft(xs,sign):
    n=len(xs)
    if n==1: return xs
    even,odd=c_fft(xs[0::2],sign),c_fft(xs[1::2],sign)
    out=[None]*n
    for k in range(n//2):
        t=c_turn(odd[k],sign*2*math.pi*k/n)
        out[k],out[k+n//2]=c_add(even[k],t),c_sub(even[k],t)
    return out
def real_spectrum(d):
    n=len(d)
    if n==2:
        return {0:d[0]+d[1],1:(d[0],-d[1]),2:d[0]-d[1]}
    half=n//2
    out={}
    z=[c_turn((d[a],-d[a+half]),-math.pi*a/n) for a in range(half)]
    f=c_fft(z,-1)
    for m in range(half):
        k=1+4*m
        if k<n: out[k]=f[m]
        else: out[2*n-k]=(f[m][0],-f[m][1])
    s=[d[a]+d[a+half] for a in range(half)]
    e=[d[a]-d[a+half] for a in range(half)]
    q=half//2
    z=[c_turn((e[a],-e[a+q]),-2*math.pi*a/n) for a in range(q)]
    f=c_fft(z,-1)
    for l in range(q):
        m=1+4*l
        if m<=half: out[2*m]=f[l]
        else: out[2*(n-m)]=(f[l][0],-f[l][1])
    sub=real_full(s)
    for l,v in sub.items(): out[4*l]=v
    return out
def real_full(s):
    n=len(s)
    if n==2: return {0:s[0]+s[1],1:s[0]-s[1]}
    half=n//2
    p=[s[a]+s[a+half] for a in range(half)]
    e=[s[a]-s[a+half] for a in range(half)]
    out={}
    for l,v in real_full(p).items(): out[2*l]=v
    q=half//2
    if q==0: return out
    z=[c_turn((e[a],-e[a+q]),-2*math.pi*a/n) for a in range(q)] if q else []
    f=c_fft(z,-1)
    for k in range(q):
        l=1+4*k
        if l<=half: out[l]=f[k]
        else: out[n-l]=(f[k][0],-f[k][1])
    return out
def real_full_back(v,n):
    if n==2: return [v[0]+v[1],v[0]-v[1]]
    half=n//2; q=half//2
    p=real_full_back({l//2:x for l,x in v.items() if l%2==0},half)
    if n==4:
        g=[v[1]]
    else:
        g=[v[1+4*k] if 1+4*k<=half else (v[n-1-4*k][0],-v[n-1-4*k][1]) for k in range(q)]
    f=c_fft(g,1)
    odd=[None]*half
    for a in range(q):
        t=c_turn(f[a],2*math.pi*a/n)
        odd[a],odd[a+q]=t[0],-t[1]
    out=[None]*n
    for a in range(half):
        out[a],out[a+half]=p[a]+odd[a],p[a]-odd[a]
    return out
def real_back(y,n):
    half=n//2
    even=real_full_back({k//2:v for k,v in y.items() if k%2==0},n)
    g=[y[1+4*m] if 1+4*m<n else (y[2*n-1-4*m][0],-y[2*n-1-4*m][1]) for m in range(half)]
    f=c_fft(g,1)
    out=[None]*n
    for a in range(half):
        t=c_turn(f[a],math.pi*a/n)
        out[a],out[a+half]=even[a]+t[0],even[a+half]-t[1]
    return out


def split_np(table):
    high = table.astype(np.float32).astype(BF)
    low = (table - high.astype(np.float64)).astype(np.float32).astype(BF)
    return np.stack([high, low])


@functools.lru_cache(None)
def tables():
    pi = np.pi
    k2 = np.arange(64)[:, None]
    b = np.arange(128)[None, :]
    c1, s1 = np.cos(pi * k2 * (2 * b + 1) / 128), np.sin(pi * k2 * (2 * b + 1) / 128)
    c2, s2 = np.cos(pi * (k2 + 1) * (2 * b + 1) / 128), np.sin(pi * (k2 + 1) * (2 * b + 1) / 128)
    cm, sm = np.cos(pi * (2 * k2 + 1) * (2 * b + 1) / 256), np.sin(pi * (2 * k2 + 1) * (2 * b + 1) / 256)
    zero = np.zeros_like(c1)
    wc = np.block([[c1, s1], [c2, -s2]])
    wc0 = np.block([[c1, zero], [zero, cm]])
    ws = np.block([[s1, -c1], [s2, c2]])
    ws0 = np.block([[s1, zero], [zero, sm]])
    w = np.stack([split_np(m) for m in (ws, ws0, wc, wc0)]).reshape(2, 2, 2, 128, 256)
    kap = np.arange(16)[:, None]
    ang = pi * kap * (2 * b + 1) / 4096
    tx = np.stack([np.cos(ang), np.sin(ang)]).astype(np.float32)
    p1 = np.arange(256)[:, None]
    d = np.arange(256)[None, :]
    cre, cim = np.cos(2 * pi * p1 * d / 512), -np.sin(2 * pi * p1 * d / 512)
    cim[0] = (-1.0) ** np.arange(256)
    cy = np.concatenate([cre, cim], 0)
    cy_fwd, cy_inv = split_np(cy), split_np(cy.T)
    r = np.arange(8)
    angy = pi * p1 * (2 * r[None, :] + 1) / 4096
    ty = np.stack([np.tile(np.cos(angy), (1, 16)), np.tile(np.sin(angy), (1, 16))]).astype(np.float32)
    p2 = np.arange(4)[None, :]
    rr = r[:, None]
    e0, e1 = pi * p2 * (2 * rr + 1) / 8, pi * (p2 + 1) * (2 * rr + 1) / 8
    em = pi * (2 * rr + 1) * (1 + 2 * p2) / 16
    z8 = np.zeros((8, 4))
    bc = (np.block([np.cos(e0), np.cos(e1)]), np.block([np.sin(e0), -np.sin(e1)]))
    bc0 = (np.block([np.cos(e0), z8]), np.block([z8, np.cos(em)]))
    bs = (np.block([np.sin(e0), np.sin(e1)]), np.block([-np.cos(e0), np.cos(e1)]))
    bs0 = (np.block([np.sin(e0), z8]), np.block([z8, np.sin(em)]))

    def wide(pair):
        return np.concatenate([np.kron(np.eye(16), part) for part in pair], 0)

    b_fwd = np.stack([np.concatenate(list(split_np(wide(m))), axis=1) for m in (bc, bc0)])
    b_inv = np.stack([split_np(wide(m).T) for m in (bc, bc0, bs, bs0)]).reshape(2, 2, 2, 128, 256)
    return w, tx, cy_fwd, cy_inv, ty, b_fwd, b_inv


def dot(x, y):
    return lax.dot_general(x, y, (((1,), (0,)), ((), ())), preferred_element_type=F32)


def dot_nt(x, y):
    return lax.dot_general(x, y, (((1,), (1,)), ((), ())), preferred_element_type=F32)


def split(x):
    high = x.astype(BF)
    return high, (x - high.astype(F32)).astype(BF)


def dot3(x, y):
    return dot(x[0], y[0]) + (dot(x[0], y[1]) + dot(x[1], y[0]))


def dot3_nt(x, y):
    return dot_nt(x[0], y[0]) + (dot_nt(x[0], y[1]) + dot_nt(x[1], y[0]))


def encode(x, y):
    top = jnp.maximum(jnp.maximum(jnp.abs(x), jnp.abs(y)), 2.0**-31)
    exponent = jnp.minimum(jnp.floor(jnp.log2(top)), 31.0)
    scale = jnp.exp2(11.0 - exponent)

    def code(v):
        return jnp.clip(jnp.round(v * scale), -4095.0, 4095.0).astype(I32)

    high = jnp.left_shift(exponent.astype(I32) + 32, 26)
    return high | jnp.left_shift(code(y) & 0x1FFF, 13) | (code(x) & 0x1FFF)


def decode(word):
    scale = jnp.exp2(lax.shift_right_logical(word, 26).astype(F32) - 43.0)
    x = lax.shift_right_arithmetic(jnp.left_shift(word, 19), 19).astype(F32)
    y = lax.shift_right_arithmetic(jnp.left_shift(word, 6), 19).astype(F32)
    return x * scale, y * scale


def place():
    slab = lax.axis_index("slab")
    cell = lax.axis_index("cell")
    return slab, cell, lax.div(slab, 8), lax.rem(slab, 8) * 2 + cell


def device_at(plane, column):
    return (plane * 8 + lax.div(column, 2), lax.rem(column, 2))


def overlap(bins, low, high):
    return jnp.maximum(jnp.minimum(bins + 1.0, high) - jnp.maximum(bins, low), 0.0)


def kernel(
    row_h, col_h, width_h, height_h, region_h, offset_h,
    w_h, tx_h, cyf_h, cyi_h, ty_h, bf_h, bi_h,
    field_x, field_y, force, sums,
    ci, co, pq, ym, yr, xb, d2, zs, s1, r1, us, vs, gs, aw, pt, s2, r2, zx, fb, pf, pr, e1, e2, es,
    w, w2, tx, cyf, cyi, ty, bf, bi, bi2,
    const_sem, in_sem, col_sem, cell_s, cell_r, a1_s, a1_r, a2_s, a2_r, f_s, f_r, e_s, e_r,
):
    slab, cell, plane, column = place()
    me = plane * 16 + column
    mine, other = cell, 1 - cell
    has_prev = jnp.logical_and(cell == 0, slab > 0)
    has_next = slab < SLABS - 1
    barrier = pltpu.get_barrier_semaphore()

    own = [
        pltpu.make_async_copy(src, ci.at[mine, k], in_sem.at[k])
        for k, src in enumerate((row_h, col_h, width_h, height_h, region_h))
    ]
    own.append(pltpu.make_async_copy(offset_h, co.at[mine], in_sem.at[5]))
    for copy in own:
        copy.start()

    def signal_at(sem, device):
        pl.semaphore_signal(sem, inc=1, device_id=device, device_id_type=MESH)

    @pl.when(has_prev)
    def _():
        signal_at(barrier, (slab - 1, 0))
        signal_at(barrier, (slab - 1, 1))

    for i in range(1, 16):
        signal_at(barrier, device_at(lax.rem(plane + i, 16), column))
        signal_at(barrier, device_at(plane, lax.rem(column + i, 16)))

    fetched = [
        pltpu.make_async_copy(src, dst, const_sem.at[k])
        for k, (src, dst) in enumerate(
            (
                (tx_h, tx), (w_h, w), (w_h.at[:, 0, 0], w2.at[:, 0:128]), (w_h.at[:, 0, 0], w2.at[:, 128:256]),
                (cyf_h, cyf), (ty_h, ty), (bf_h, bf), (bi_h, bi),
                (bi_h.at[:, 0, 0], bi2.at[:, 0:128]), (bi_h.at[:, 0, 0], bi2.at[:, 128:256]), (cyi_h, cyi),
            )
        )
    ]
    for copy in fetched:
        copy.start()
    for copy in own:
        copy.wait()

    low_row = slab * 16 + cell * 8

    def cell_row_of(slot, k, which):
        return ci[slot, which, k : k + 1, :]

    def make_cells(slot):
        bins = lax.broadcasted_iota(I32, (128, 128), 0).astype(F32)
        rows = (lax.broadcasted_iota(I32, (8, 128), 0) + low_row).astype(F32)
        for k in range(4):
            at = slice(128 * k, 128 * k + 128)
            far = slice(512 + 128 * k, 640 + 128 * k)
            col = cell_row_of(slot, k, 1)
            high_bits = lax.shift_right_logical(col, 7)
            low_bits = (col - high_bits * 128).astype(F32)
            start = co[slot, 0:1, at]
            end = start + cell_row_of(slot, k, 2).astype(F32)
            reach = bins - low_bits
            pq[slot, :, at] = overlap(reach, start, end).astype(BF)
            pq[slot, :, far] = overlap(reach + 128.0, start, end).astype(BF)
            start = co[slot, 1:2, at]
            end = start + cell_row_of(slot, k, 3).astype(F32)
            got = overlap(rows - cell_row_of(slot, k, 0).astype(F32), start, end)
            region = cell_row_of(slot, k, 4)
            parts = jnp.concatenate([jnp.where(region == g, got, 0.0) for g in range(REGIONS)], axis=0)
            yr[slot, :, at] = parts.astype(BF).astype(F32)
            for a in range(16):
                to = slice(32 * a, 32 * a + 32)
                ym[to, at] = jnp.where(high_bits == a, parts, 0.0).astype(BF)
                ym[to, far] = jnp.where(high_bits == a - 1, parts, 0.0).astype(BF)

    def add_density(slot, fresh):
        got = dot_nt(ym[...], pq[slot])
        d2[...] = got if fresh else d2[...] + got

    def send(src, dst, s_sem, r_sem, device):
        return pltpu.make_async_remote_copy(
            src_ref=src, dst_ref=dst, send_sem=s_sem, recv_sem=r_sem, device_id=device, device_id_type=MESH
        )

    make_cells(mine)
    pl.semaphore_wait(barrier, 30 + has_next.astype(I32))
    partner = (slab, other)
    give = [
        send(ci.at[mine], ci.at[mine], cell_s.at[0], cell_r.at[0, mine], partner),
        send(co.at[mine], co.at[mine], cell_s.at[1], cell_r.at[1, mine], partner),
    ]
    give_next = [
        send(ci.at[mine], ci.at[2 + mine], cell_s.at[2], cell_r.at[0, 2 + mine], (slab + 1, 0)),
        send(co.at[mine], co.at[2 + mine], cell_s.at[3], cell_r.at[1, 2 + mine], (slab + 1, 0)),
    ]
    for copy in give:
        copy.start()

    @pl.when(has_next)
    def _():
        for copy in give_next:
            copy.start()

    for i in range(1, 16):
        signal_at(col_sem, device_at(plane, lax.rem(column + i, 16)))

    def arrive(slot):
        send(ci.at[slot], ci.at[slot], cell_s.at[0], cell_r.at[0, slot], partner).wait_recv()
        send(co.at[slot], co.at[slot], cell_s.at[1], cell_r.at[1, slot], partner).wait_recv()

    add_density(mine, True)
    arrive(other)
    make_cells(other)
    add_density(other, False)

    @pl.when(has_prev)
    def _():
        for k in range(2):
            arrive(2 + k)
            make_cells(2 + k)
            add_density(2 + k, False)

    def tally(i, carry):
        excess, area = carry
        got = d2[pl.ds(pl.multiple_of(i * 64, 64), 64), :].reshape(8, 8, 128)
        return excess + jnp.sum(jnp.maximum(got - 1.0, 0.0), axis=0), area + jnp.sum(got, axis=0)

    zero8 = jnp.zeros((8, 128), F32)
    excess, area = lax.fori_loop(0, 8, tally, (zero8, zero8))
    lane = lax.broadcasted_iota(I32, (1, 128), 1)
    first_group = lane < 32

    fetched[0].wait()

    def x_chunk(i, carry):
        at = pl.multiple_of(i * 16, 16)
        got = real_spectrum([d2[pl.ds(pl.multiple_of(32 * a + at, 16), 16), :] for a in range(16)])
        for kap in range(16):
            if kap == 0:
                pair = (got[0], got[16])
            else:
                (re, im), c, s = got[kap], tx[0, kap : kap + 1, :], tx[1, kap : kap + 1, :]
                pair = (re * c + im * s, im * c - re * s)
            for half, value in enumerate(pair):
                parts = split(value)
                for k in range(2):
                    zs[k, pl.ds(pl.multiple_of(32 * kap + at, 16), 16), 128 * half : 128 * half + 128] = parts[k]
        return carry

    lax.fori_loop(0, 2, x_chunk, 0)
    fetched[1].wait()
    table, first = (w[1, 0, 0], w[1, 0, 1]), (w[1, 1, 0], w[1, 1, 1])
    got = dot3_nt(table, (zs[0, :, 0:256], zs[1, :, 0:256]))
    fixed = dot3_nt(first, (zs[0, 0:128, 0:256], zs[1, 0:128, 0:256]))
    tiles = [got[:, 128 * t : 128 * t + 128] for t in range(4)]
    tiles[0] = jnp.where(first_group, fixed, tiles[0])
    for t in range(2):
        s1[128 * t : 128 * t + 128, :] = encode(tiles[t], tiles[t + 2])

    pl.semaphore_wait(col_sem, 15)
    py, px = lax.div(plane, 4), lax.rem(plane, 4)
    z, core = lax.div(column, 4) * 2 + cell, lax.rem(lax.div(column, 2), 2)
    ys = [lax.rem(py + k, 4) for k in range(4)]
    xs = [lax.rem(px + k, 4) for k in range(4)]
    hops = [0, 1, 2, 1]
    near = sorted(((dy, dx, dc) for dy in range(4) for dx in range(4) for dc in range(2)), key=lambda d: -(hops[d[0]] + hops[d[1]] + 0.5 * d[2]))

    def exchange(at, src, dst, s_sem, r_sem):
        def ring(dz, skip_self):
            there = lax.rem(z + dz, 8)
            zh, zl = lax.div(there, 2), lax.rem(there, 2)
            for dy, dx, dc in near:
                if skip_self and dy == dx == dc == 0:
                    continue
                core_to = core if dc == 0 else 1 - core
                plane_to = ys[dy] * 4 + xs[dx]
                to = plane_to * 16 + (zh * 4 + zl + core_to * 2)
                send(at(src, to), at(dst, me), s_sem, r_sem, (plane_to * 8 + (zh * 2 + core_to), zl)).start()

        def step(i, carry):
            ring(4 + lax.div(i + 1, 2) * (1 - 2 * lax.rem(i, 2)), False)
            return carry

        lax.fori_loop(0, 7, step, 0)
        ring(0, True)

    def row_of(ref, m):
        return ref.at[pl.ds(m, 1)]

    def rows_of(ref, m):
        return ref.at[:, pl.ds(m, 1)]

    exchange(row_of, s1, r1, a1_s, a1_r)
    r1[pl.ds(me, 1), :] = s1[pl.ds(me, 1), :]

    tile, k2c = lax.div(me, 128), lax.rem(me, 128)
    lower = k2c < 64
    group = lax.div(lane, 32)
    order = lax.rem(lane, 8)

    def q_of(h):
        kap = 4 * (tile + 2 * h) + group
        return jnp.where(
            kap == 0,
            jnp.where(lower, 32 * k2c, 16 + 32 * (k2c - 64)),
            jnp.where(lower, kap + 32 * k2c, 32 - kap + 32 * (k2c - 64)),
        )

    qs = [q_of(h) for h in range(2)]

    def weigh(i, carry):
        at = pl.multiple_of(i * 16, 16)
        p1 = lax.broadcasted_iota(I32, (16, 128), 0) + at
        up = order < 4
        p = jnp.where(up, p1 + 512 * order, 512 - p1 + 512 * (order - 4))
        p = jnp.where(jnp.logical_and(p1 == 0, jnp.logical_not(up)), 256 + 512 * (order - 4), p)
        p_float = p.astype(F32)
        pt[pl.ds(at, 16), :] = p_float
        for h in range(2):
            q_float = qs[h].astype(F32)
            k2 = p_float * p_float + q_float * q_float
            scale = jnp.where(p == 0, 1.0 / M, 2.0 / M) * jnp.where(qs[h] == 0, 1.0 / M, 2.0 / M) * (1.0 / STEP)
            aw[pl.ds(256 * h + at, 16), :] = jnp.where(k2 == 0.0, 0.0, scale / jnp.where(k2 == 0.0, 1.0, k2))
        return carry

    lax.fori_loop(0, 16, weigh, 0)

    def make_profiles(slot):
        def block(a, carry):
            to = pl.ds(pl.multiple_of(a * 128, 128), 128)
            for k in range(4):
                at = slice(128 * k, 128 * k + 128)
                high_bits = lax.shift_right_logical(cell_row_of(slot, k, 1), 7)
                first = (high_bits == a).astype(F32).astype(BF)
                second = (high_bits == a - 1).astype(F32).astype(BF)
                xb[slot, to, at] = pq[slot, :, at] * first + pq[slot, :, 512 + 128 * k : 640 + 128 * k] * second
            return carry

        lax.fori_loop(0, 16, block, 0)

    make_profiles(mine)
    make_profiles(other)

    @pl.when(has_prev)
    def _():
        for k in range(2):
            make_profiles(2 + k)

    for copy in fetched[2:]:
        copy.wait()
    whole = send(s1.at[pl.ds(0, 255)], r1.at[pl.ds(0, 255)], a1_s, a1_r, partner)
    whole.wait_recv()
    whole.wait_send()

    high, low = zip(*(split(v) for v in decode(r1[...])))
    whole = (jnp.concatenate(high, axis=1), jnp.concatenate(low, axis=1))
    us[...] = dot3((cyf[0], cyf[1]), whole)

    def y_chunk(i, carry):
        at = pl.multiple_of(i * 16, 16)
        c, s = ty[0, pl.ds(at, 16), :], ty[1, pl.ds(at, 16), :]
        for h in range(2):
            lanes = slice(128 * h, 128 * h + 128)
            re, im = us[pl.ds(at, 16), lanes], us[pl.ds(256 + at, 16), lanes]
            for half, value in enumerate((re * c + im * s, im * c - re * s)):
                parts = split(value)
                for k in range(2):
                    vs[k, pl.ds(256 * h + at, 16), 128 * half : 128 * half + 128] = parts[k]
        return carry

    lax.fori_loop(0, 16, y_chunk, 0)

    def y_out(rows, table):
        got = dot(vs[0, rows], table)
        return got[:, 0:128] + (got[:, 128:256] + dot(vs[1, rows], table[:, 0:128]))

    gs[...] = y_out(slice(0, 512), bf[0])
    top_row = lax.broadcasted_iota(I32, (16, 1), 0) == 0
    for h in range(2):
        at = slice(256 * h, 256 * h + 16)
        gs[at, :] = jnp.where(top_row, y_out(at, bf[1]), gs[at, :])

    q_floats = [q.astype(F32) for q in qs]

    def scale_chunk(i, energy):
        at = pl.multiple_of(i * 16, 16)
        p_float = pt[pl.ds(at, 16), :]
        for h in range(2):
            value = gs[pl.ds(256 * h + at, 16), :]
            weighted = value * aw[pl.ds(256 * h + at, 16), :]
            work = weighted * value
            energy = energy + (work[0:8] + work[8:16])
            for f, part in enumerate((weighted * q_floats[h], weighted * p_float)):
                parts = split(part)
                for k in range(2):
                    vs[f, pl.ds(256 * h + at, 16), 128 * k : 128 * k + 128] = parts[k]
        return energy

    energy = lax.fori_loop(0, 16, scale_chunk, zero8)

    for f in range(2):
        us[...] = dot(vs[f], bi2[f]) + dot(vs[f, :, 0:128], bi[f, 0, 1])
        for h in range(2):
            at = slice(256 * h, 256 * h + 16)
            fixed = dot3((vs[f, at, 0:128], vs[f, at, 128:256]), (bi[f, 1, 0], bi[f, 1, 1]))
            us[at, :] = jnp.where(top_row, fixed, us[at, :])

        def back_chunk(i, carry, f=f):
            at = pl.multiple_of(i * 16, 16)
            c, s = ty[0, pl.ds(at, 16), :], ty[1, pl.ds(at, 16), :]
            for h in range(2):
                re, im = us[pl.ds(256 * h + at, 16), 0:128], us[pl.ds(256 * h + at, 16), 128:256]
                lanes = slice(256 * f + 128 * h, 256 * f + 128 * h + 128)
                for half, value in enumerate((re * c - im * s, re * s + im * c)):
                    parts = split(value)
                    for k in range(2):
                        zs[k, pl.ds(256 * half + at, 16), lanes] = parts[k]
            return carry

        lax.fori_loop(0, 16, back_chunk, 0)
    for f in range(2):
        lanes = slice(256 * f, 256 * f + 256)
        got = dot3((cyi[0], cyi[1]), (zs[0, :, lanes], zs[1, :, lanes]))
        s2[f] = encode(got[:, 0:128], got[:, 128:256])

    exchange(rows_of, s2, r2, a2_s, a2_r)
    r2[:, pl.ds(me, 1), :] = s2[:, pl.ds(me, 1), :]

    def total(x):
        return jnp.sum(jnp.sum(x, axis=1, keepdims=True), axis=0, keepdims=True)

    row = jnp.where(
        lane == 0, total(excess), jnp.where(lane == 1, total(area), total(energy) * (1.0 / (STEP * M * M)))
    )
    es[0] = row
    e1[plane] = row
    for i in range(1, 16):
        send(es.at[0], e1.at[plane], e_s.at[0], e_r.at[0], device_at(lax.rem(plane + i, 16), column)).start()
    whole = send(s2.at[:, pl.ds(0, 255)], r2.at[:, pl.ds(0, 255)], a2_s, a2_r, partner)
    whole.wait_recv()
    whole.wait_send()
    sums_wait = send(e1.at[pl.ds(0, 15)], e1.at[pl.ds(0, 15)], e_s.at[0], e_r.at[0], partner)
    sums_wait.wait_recv()
    sums_wait.wait_send()
    row = jnp.sum(e1[...], axis=0)
    es[1] = row
    e2[column] = row
    for i in range(1, 16):
        send(es.at[1], e2.at[column], e_s.at[1], e_r.at[1], device_at(plane, lax.rem(column + i, 16))).start()

    for f, out in enumerate((field_x, field_y)):
        for t in range(2):
            for h, value in enumerate(decode(r2[f, 128 * t : 128 * t + 128, :])):
                parts = split(value.T)
                for k in range(2):
                    rows = slice(128 * (t + 2 * h), 128 * (t + 2 * h) + 128)
                    zx[rows, 128 * k : 128 * k + 128] = parts[k]
        us[...] = dot(zx[...], w2[f]) + dot(zx[:, 0:128], w[f, 0, 1])
        us[0:32, :] = dot3((zx[0:32, 0:128], zx[0:32, 128:256]), (w[f, 1, 0], w[f, 1, 1]))

        def out_chunk(i, carry, f=f, out=out):
            at = pl.multiple_of(i * 16, 16)
            got = {}
            for kap in range(16):
                rows = pl.ds(pl.multiple_of(32 * kap + at, 16), 16)
                re, im = us[rows, 0:128], us[rows, 128:256]
                if kap == 0:
                    got[0], got[16] = re, im
                else:
                    c, s = tx[0, kap : kap + 1, :], tx[1, kap : kap + 1, :]
                    got[kap] = (re * c - im * s, re * s + im * c)
            for a, value in enumerate(real_back(got, 16)):
                lanes = slice(128 * a, 128 * a + 128)
                out[2 * i, :, lanes] = value[0:8]
                out[2 * i + 1, :, lanes] = value[8:16]
                fb[pl.ds(pl.multiple_of(32 * f + at, 16), 16), lanes] = value.astype(BF)
            return carry

        lax.fori_loop(0, 2, out_chunk, 0)

    def push(slot):
        got = dot(fb[...], xb[slot])
        for f in range(2):
            pf[slot, f : f + 1, :] = jnp.sum(got[32 * f : 32 * f + 32, :] * yr[slot], axis=0, keepdims=True)

    def give_back(slot, device, sem, into):
        return send(pf.at[slot], pr.at[into], f_s.at[sem], f_r.at[into], device)

    push(other)
    give_back(other, partner, 0, 0).start()

    @pl.when(has_prev)
    def _():
        for k in range(2):
            push(2 + k)
            give_back(2 + k, (slab - 1, k), 1 + k, 1).start()

    push(mine)

    @pl.when(jnp.logical_not(has_next))
    def _():
        pr[1] = jnp.zeros((2, CELLS_DEV), F32)

    give_back(other, partner, 0, 0).wait_recv()

    @pl.when(has_next)
    def _():
        give_back(other, partner, 0, 1).wait_recv()

    force[...] = pf[mine] + pr[0] + pr[1]

    send(e2.at[pl.ds(0, 15)], e2.at[pl.ds(0, 15)], e_s.at[1], e_r.at[1], partner).wait()
    sums[...] = jnp.sum(e2[...], axis=0)

    give_back(other, partner, 0, 0).wait_send()
    for copy in give:
        copy.wait_send()

    @pl.when(has_prev)
    def _():
        for k in range(2):
            give_back(2 + k, (slab - 1, k), 1 + k, 1).wait_send()

    @pl.when(has_next)
    def _():
        for copy in give_next:
            copy.wait_send()


def finish(field_x, field_y, force, sums, out_x, out_y, out_force, energy, overflow, sem):
    copies = [
        pltpu.make_async_copy(src, dst, sem.at[k])
        for k, (src, dst) in enumerate(((field_x, out_x), (field_y, out_y), (force, out_force)))
    ]
    for copy in copies:
        copy.start()
    row = sums[...]
    energy[...] = row[:, 2:3]
    overflow[...] = row[:, 0:1] / row[:, 1:2]
    for copy in copies:
        copy.wait()


def body(cell_row, cell_col, cell_width, cell_height, cell_region, cell_offset):
    consts = [jnp.asarray(t) for t in tables()]
    whole = [v.reshape(4, 128) for v in (cell_row, cell_col, cell_width, cell_height, cell_region)]
    vmem = pl.BlockSpec(memory_space=pltpu.VMEM)
    hbm = pl.BlockSpec(memory_space=pltpu.HBM)
    V = pltpu.VMEM
    D = pltpu.SemaphoreType.DMA
    scratch = [
        V((4, 5, 4, 128), I32),
        V((4, 2, CELLS_DEV), F32),
        V((4, 128, 1024), BF),
        V((512, 1024), BF),
        V((4, 32, CELLS_DEV), F32),
        V((4, M, CELLS_DEV), BF),
        V((512, 128), F32),
        V((2, 512, 512), BF),
        V((256, 128), I32),
        V((256, 128), I32),
        V((512, 256), F32),
        V((2, 512, 256), BF),
        V((512, 128), F32),
        V((512, 128), F32),
        V((256, 128), F32),
        V((2, 256, 128), I32),
        V((2, 256, 128), I32),
        V((512, 256), BF),
        V((64, M), BF),
        V((4, 2, CELLS_DEV), F32),
        V((2, 2, CELLS_DEV), F32),
        V((16, 1, 128), F32),
        V((16, 1, 128), F32),
        V((2, 1, 128), F32),
        V((2, 2, 2, 128, 256), BF),
        V((2, 256, 256), BF),
        V((2, 16, 128), F32),
        V((2, 512, 256), BF),
        V((2, 256, 512), BF),
        V((2, 256, 128), F32),
        V((2, 256, 256), BF),
        V((2, 2, 2, 128, 256), BF),
        V((2, 256, 256), BF),
        D((11,)), D((6,)),
        pltpu.SemaphoreType.REGULAR,
        D((4,)), D((2, 4)),
        D, D, D, D,
        D((3,)), D((2,)),
        D((2,)), D((2,)),
    ]
    field = (REGIONS, 8, M)
    results = pl.pallas_call(
        kernel,
        out_shape=(V(field, F32), V(field, F32), V((2, CELLS_DEV), F32), V((1, 128), F32)),
        in_specs=[hbm] * (6 + len(consts)),
        out_specs=(vmem,) * 4,
        scratch_shapes=scratch,
        compiler_params=pltpu.CompilerParams(
            collective_id=0, has_side_effects=True, vmem_limit_bytes=66300000
        ),
        name="placement",
    )(*whole, cell_offset, *consts)
    S = jax.ShapeDtypeStruct
    field_x, field_y, force, energy, overflow = pl.pallas_call(
        finish,
        out_shape=(S(field, F32), S(field, F32), S((2, CELLS_DEV), F32), S((1, 1), F32), S((1, 1), F32)),
        in_specs=[vmem] * 4,
        out_specs=(hbm, hbm, hbm, vmem, vmem),
        scratch_shapes=[D((3,))],
        compiler_params=pltpu.CompilerParams(vmem_limit_bytes=4 * 1024 * 1024),
        name="finish",
    )(*results)
    return (field_x, field_y, force, energy.reshape(()), overflow.reshape(()))


def solution(mesh):
    both = ("slab", "cell")
    placed = (P(both),) * 5 + (P(None, both),)
    return jax.shard_map(
        body,
        mesh=mesh,
        in_specs=placed,
        out_specs=(P(None, both, None), P(None, both, None), P(None, both), P(), P()),
        check_vma=False,
    )
```

time: 70.5 us -> 46.2 us (0.66)
  Pallas kernels: 57.8 us -> 45.5 us
  local copies, waits for them, and re-layouts: 9.2 us -> 0 us
  between operations: 3.13 us -> 0.64 us
    pallas_call x1 -> x2, Pallas kernels: 57.8 us -> 45.5 us  [the longest x1 44.1 us: body(): pl.pallas_call(kernel, out_shape=(V(field, F32), V(field, F32), V((2, CEL...]
    unnamed x17 -> x0, local copies, waits for them, and re-layouts: 6.41 us -> none
    slice x2 -> x0, local copies, waits for them, and re-layouts: 2.15 us -> none  [the longest x1 1.38 us: body(): overflow = sums[0, 0] / sums[0, 1]]
where the time goes in v2:
time: 46.2 us; the launch traced here: 46.1 us
  Pallas kernels  45.5 us (98%)
  between operations  0.64 us (1%)
    pallas_call x1, Pallas kernels, body(): pl.pallas_call(kernel, out_shape=(V(field, F32), V(field, F32), V((2, CEL...  44.1 us
    pallas_call x1, Pallas kernels, body(): pl.pallas_call(finish, out_shape=(S(field, F32), S(field, F32), S((2, CEL...  1.33 us

profile of v2, /device:TPU:1, one launch (start us, length us, event | category | flops | bytes accessed | tf_op | source)
XLA Modules:
  0.0 46.1 jit_solution(388368005540097361)
XLA Ops:
  0.6 44.1 %placement.1 = (f32[4,8,2048]{2,1,0:T(8,128)S(1)}, f32[4,8,2048]{2,1,0:T(8,128)S(1)}, f32[2,512]{1,0:T(2,128)S(1)}, f32[1,128]{1,0:T(1,128)S(1)}) custom-call(s32[4,128]{1,0:T(4,128)} %bitcast.7, s32[4,128]{1,0:T(4,128)} %bitcast.8, s32[4,128]{1,0:T(4,128)} %bitcast.9, s32[4,128]{1,0:T(4,128)} %bitcast.10, s32[4,128]{1,0:T(4,128)} %bitcast.11, ...), custom_call_target="tpu_custom_call" | custom-call | tf_op jit(solution)/shard_map/placement/pallas_call | solution.py:717
  44.8 1.3 %finish.1 = (f32[4,8,2048]{2,1,0:T(8,128)}, f32[4,8,2048]{2,1,0:T(8,128)}, f32[2,512]{1,0:T(2,128)}, f32[1,1]{1,0:T(1,128)}, f32[1,1]{1,0:T(1,128)}) custom-call(f32[4,8,2048]{2,1,0:T(8,128)S(1)} %get-tuple-element.14.field_x, f32[4,8,2048]{2,1,0:T(8,128)S(1)} %get-tuple-element.15.field_y, f32[2,512]{1,0:T(2,128)S(1)} %get-tuple-element.16.force, ...), custom_call_target="tpu_custom_call" | custom-call | tf_op jit(solution)/shard_map/finish/pallas_call | solution.py:729

commit v3 on v2

--- a/solution.py
+++ b/solution.py
@@ -140,11 +140,12 @@
     d = np.arange(256)[None, :]
     cre, cim = np.cos(2 * pi * p1 * d / 512), -np.sin(2 * pi * p1 * d / 512)
     cim[0] = (-1.0) ** np.arange(256)
-    cy = np.concatenate([cre, cim], 0)
+    cy = np.concatenate([cre, cim], 0)[:, np.arange(256).reshape(128, 2).T.reshape(-1)]
+    ours = np.arange(128).reshape(4, 4, 2, 4).transpose(0, 2, 1, 3).reshape(-1)
     cy_fwd, cy_inv = split_np(cy), split_np(cy.T)
     r = np.arange(8)
     angy = pi * p1 * (2 * r[None, :] + 1) / 4096
-    ty = np.stack([np.tile(np.cos(angy), (1, 16)), np.tile(np.sin(angy), (1, 16))]).astype(np.float32)
+    ty = np.stack([np.tile(np.cos(angy), (1, 16)), np.tile(np.sin(angy), (1, 16))])[:, :, ours].astype(np.float32)
     p2 = np.arange(4)[None, :]
     rr = r[:, None]
     e0, e1 = pi * p2 * (2 * rr + 1) / 8, pi * (p2 + 1) * (2 * rr + 1) / 8
@@ -156,7 +157,7 @@
     bs0 = (np.block([np.sin(e0), z8]), np.block([z8, np.sin(em)]))
 
     def wide(pair):
-        return np.concatenate([np.kron(np.eye(16), part) for part in pair], 0)
+        return np.concatenate([np.kron(np.eye(16), part)[ours] for part in pair], 0)
 
     b_fwd = np.stack([np.concatenate(list(split_np(wide(m))), axis=1) for m in (bc, bc0)])
     b_inv = np.stack([split_np(wide(m).T) for m in (bc, bc0, bs, bs0)]).reshape(2, 2, 2, 128, 256)
@@ -203,6 +204,15 @@
     return x * scale, y * scale
 
 
+@functools.lru_cache(None)
+def send_order():
+    rng = np.random.default_rng(0)
+    every = [(dz, dy, dx, dc) for dz in range(8) for dy in range(4) for dx in range(4) for dc in range(2)]
+    every = [d for d in every if any(d)]
+    hops = {d: min(d[0], 8 - d[0]) + min(d[1], 4 - d[1]) + min(d[2], 4 - d[2]) + 0.5 * d[3] for d in every}
+    return sorted(every, key=lambda d: (-hops[d], rng.random()))
+
+
 def place():
     slab = lax.axis_index("slab")
     cell = lax.axis_index("cell")
@@ -221,9 +231,9 @@
     row_h, col_h, width_h, height_h, region_h, offset_h,
     w_h, tx_h, cyf_h, cyi_h, ty_h, bf_h, bi_h,
     field_x, field_y, force, sums,
-    ci, co, pq, ym, yr, xb, d2, zs, s1, r1, us, vs, gs, aw, pt, s2, r2, zx, fb, pf, pr, e1, e2, es,
+    ci, co, pq, ym, yr, d2, zs, s1, r1, us, vs, gs, aw, pt, s2, r2, zx, fb, pf, pr, e1, e2, es,
     w, w2, tx, cyf, cyi, ty, bf, bi, bi2,
-    const_sem, in_sem, col_sem, cell_s, cell_r, a1_s, a1_r, a2_s, a2_r, f_s, f_r, e_s, e_r,
+    const_sem, in_sem, met, cell_s, cell_r, a1_s, a1_r, a2_s, a2_r, f_s, f_r, e_s, e_r,
 ):
     slab, cell, plane, column = place()
     me = plane * 16 + column
@@ -248,9 +258,15 @@
         signal_at(barrier, (slab - 1, 0))
         signal_at(barrier, (slab - 1, 1))
 
-    for i in range(1, 16):
-        signal_at(barrier, device_at(lax.rem(plane + i, 16), column))
-        signal_at(barrier, device_at(plane, lax.rem(column + i, 16)))
+    py, px = lax.div(plane, 4), lax.rem(plane, 4)
+    z, core = lax.div(column, 4) * 2 + cell, lax.rem(lax.div(column, 2), 2)
+    ys = [lax.rem(py + k, 4) for k in range(4)]
+    xs = [lax.rem(px + k, 4) for k in range(4)]
+
+    plane_peers = [device_at(lax.rem(plane + i, 16), column) for i in range(1, 16)]
+    column_peers = [device_at(plane, lax.rem(column + i, 16)) for i in range(1, 16)]
+    for device in plane_peers + column_peers:
+        signal_at(barrier, device)
 
     fetched = [
         pltpu.make_async_copy(src, dst, const_sem.at[k])
@@ -272,41 +288,37 @@
     def cell_row_of(slot, k, which):
         return ci[slot, which, k : k + 1, :]
 
-    def make_cells(slot):
+    def make_cells(slot, halves, masked):
         bins = lax.broadcasted_iota(I32, (128, 128), 0).astype(F32)
-        rows = (lax.broadcasted_iota(I32, (8, 128), 0) + low_row).astype(F32)
+        line = lax.broadcasted_iota(I32, (16, 128), 0)
+        rows = (jnp.bitwise_and(line, 3) + low_row).astype(F32)
+        region_of = lax.shift_right_logical(line, 2)
         for k in range(4):
             at = slice(128 * k, 128 * k + 128)
-            far = slice(512 + 128 * k, 640 + 128 * k)
             col = cell_row_of(slot, k, 1)
             high_bits = lax.shift_right_logical(col, 7)
             low_bits = (col - high_bits * 128).astype(F32)
             start = co[slot, 0:1, at]
             end = start + cell_row_of(slot, k, 2).astype(F32)
             reach = bins - low_bits
-            pq[slot, :, at] = overlap(reach, start, end).astype(BF)
-            pq[slot, :, far] = overlap(reach + 128.0, start, end).astype(BF)
+            pq[slot, 0:128, at] = overlap(reach, start, end).astype(BF)
+            pq[slot, 128:256, at] = overlap(reach + 128.0, start, end).astype(BF)
             start = co[slot, 1:2, at]
             end = start + cell_row_of(slot, k, 3).astype(F32)
-            got = overlap(rows - cell_row_of(slot, k, 0).astype(F32), start, end)
-            region = cell_row_of(slot, k, 4)
-            parts = jnp.concatenate([jnp.where(region == g, got, 0.0) for g in range(REGIONS)], axis=0)
-            yr[slot, :, at] = parts.astype(BF).astype(F32)
-            for a in range(16):
-                to = slice(32 * a, 32 * a + 32)
-                ym[to, at] = jnp.where(high_bits == a, parts, 0.0).astype(BF)
-                ym[to, far] = jnp.where(high_bits == a - 1, parts, 0.0).astype(BF)
-
-    def add_density(slot, fresh):
-        got = dot_nt(ym[...], pq[slot])
-        d2[...] = got if fresh else d2[...] + got
+            reach = rows - cell_row_of(slot, k, 0).astype(F32)
+            here = cell_row_of(slot, k, 4) == region_of
+            for half in range(halves):
+                got = jnp.where(here, overlap(reach + 4.0 * half, start, end), 0.0)
+                yr[slot, 16 * half : 16 * half + 16, at] = got.astype(BF).astype(F32)
+                for a in range(16):
+                    to = slice(256 * half + 16 * a, 256 * half + 16 * a + 16)
+                    masked[to, at] = jnp.where(high_bits == a, got, 0.0).astype(BF)
 
     def send(src, dst, s_sem, r_sem, device):
         return pltpu.make_async_remote_copy(
             src_ref=src, dst_ref=dst, send_sem=s_sem, recv_sem=r_sem, device_id=device, device_id_type=MESH
         )
 
-    make_cells(mine)
     pl.semaphore_wait(barrier, 30 + has_next.astype(I32))
     partner = (slab, other)
     give = [
@@ -325,41 +337,47 @@
         for copy in give_next:
             copy.start()
 
-    for i in range(1, 16):
-        signal_at(col_sem, device_at(plane, lax.rem(column + i, 16)))
+    for device in column_peers:
+        signal_at(met, device)
 
     def arrive(slot):
         send(ci.at[slot], ci.at[slot], cell_s.at[0], cell_r.at[0, slot], partner).wait_recv()
         send(co.at[slot], co.at[slot], cell_s.at[1], cell_r.at[1, slot], partner).wait_recv()
 
-    add_density(mine, True)
+    make_cells(mine, 2, ym.at[0])
+    d2[...] = dot_nt(ym[0], pq[mine])
     arrive(other)
-    make_cells(other)
-    add_density(other, False)
+    make_cells(other, 2, ym.at[0])
+    d2[...] += dot_nt(ym[0], pq[other])
 
     @pl.when(has_prev)
     def _():
         for k in range(2):
             arrive(2 + k)
-            make_cells(2 + k)
-            add_density(2 + k, False)
-
-    def tally(i, carry):
-        excess, area = carry
-        got = d2[pl.ds(pl.multiple_of(i * 64, 64), 64), :].reshape(8, 8, 128)
-        return excess + jnp.sum(jnp.maximum(got - 1.0, 0.0), axis=0), area + jnp.sum(got, axis=0)
+            make_cells(2 + k, 1, ym.at[k])
+        d2[0:256, :] += dot_nt(ym[0, 0:256], pq[2]) + dot_nt(ym[1, 0:256], pq[3])
 
     zero8 = jnp.zeros((8, 128), F32)
-    excess, area = lax.fori_loop(0, 8, tally, (zero8, zero8))
     lane = lax.broadcasted_iota(I32, (1, 128), 1)
     first_group = lane < 32
 
     fetched[0].wait()
 
-    def x_chunk(i, carry):
-        at = pl.multiple_of(i * 16, 16)
-        got = real_spectrum([d2[pl.ds(pl.multiple_of(32 * a + at, 16), 16), :] for a in range(16)])
+    excess = area = zero8
+    for i in range(2):
+        here = []
+        for a in range(16):
+            at = 256 * i + 16 * a
+            value = d2[at : at + 16, 0:128]
+            if a:
+                value = value + d2[at - 16 : at, 128:256]
+            here.append(value)
+            over = jnp.maximum(value - 1.0, 0.0)
+            excess = excess + (over[0:8] + over[8:16])
+            area = area + (value[0:8] + value[8:16])
+        got = real_spectrum(here)
         for kap in range(16):
+            at = slice(32 * kap + 16 * i, 32 * kap + 16 * i + 16)
             if kap == 0:
                 pair = (got[0], got[16])
             else:
@@ -368,54 +386,30 @@
             for half, value in enumerate(pair):
                 parts = split(value)
                 for k in range(2):
-                    zs[k, pl.ds(pl.multiple_of(32 * kap + at, 16), 16), 128 * half : 128 * half + 128] = parts[k]
-        return carry
-
-    lax.fori_loop(0, 2, x_chunk, 0)
+                    zs[k, at, 128 * half : 128 * half + 128] = parts[k]
     fetched[1].wait()
     table, first = (w[1, 0, 0], w[1, 0, 1]), (w[1, 1, 0], w[1, 1, 1])
-    got = dot3_nt(table, (zs[0, :, 0:256], zs[1, :, 0:256]))
-    fixed = dot3_nt(first, (zs[0, 0:128, 0:256], zs[1, 0:128, 0:256]))
+    got = dot3_nt(table, (zs[0], zs[1]))
+    fixed = dot3_nt(first, (zs[0, 0:128], zs[1, 0:128]))
     tiles = [got[:, 128 * t : 128 * t + 128] for t in range(4)]
     tiles[0] = jnp.where(first_group, fixed, tiles[0])
     for t in range(2):
         s1[128 * t : 128 * t + 128, :] = encode(tiles[t], tiles[t + 2])
 
-    pl.semaphore_wait(col_sem, 15)
-    py, px = lax.div(plane, 4), lax.rem(plane, 4)
-    z, core = lax.div(column, 4) * 2 + cell, lax.rem(lax.div(column, 2), 2)
-    ys = [lax.rem(py + k, 4) for k in range(4)]
-    xs = [lax.rem(px + k, 4) for k in range(4)]
-    hops = [0, 1, 2, 1]
-    near = sorted(((dy, dx, dc) for dy in range(4) for dx in range(4) for dc in range(2)), key=lambda d: -(hops[d[0]] + hops[d[1]] + 0.5 * d[2]))
-
-    def exchange(at, src, dst, s_sem, r_sem):
-        def ring(dz, skip_self):
-            there = lax.rem(z + dz, 8)
-            zh, zl = lax.div(there, 2), lax.rem(there, 2)
-            for dy, dx, dc in near:
-                if skip_self and dy == dx == dc == 0:
-                    continue
-                core_to = core if dc == 0 else 1 - core
-                plane_to = ys[dy] * 4 + xs[dx]
-                to = plane_to * 16 + (zh * 4 + zl + core_to * 2)
-                send(at(src, to), at(dst, me), s_sem, r_sem, (plane_to * 8 + (zh * 2 + core_to), zl)).start()
-
-        def step(i, carry):
-            ring(4 + lax.div(i + 1, 2) * (1 - 2 * lax.rem(i, 2)), False)
-            return carry
-
-        lax.fori_loop(0, 7, step, 0)
-        ring(0, True)
-
-    def row_of(ref, m):
-        return ref.at[pl.ds(m, 1)]
-
-    def rows_of(ref, m):
-        return ref.at[:, pl.ds(m, 1)]
-
-    exchange(row_of, s1, r1, a1_s, a1_r)
-    r1[pl.ds(me, 1), :] = s1[pl.ds(me, 1), :]
+    pl.semaphore_wait(met, 15)
+    zs_there = [lax.rem(z + k, 8) for k in range(8)]
+    z_parts = [(lax.div(k, 2), lax.rem(k, 2)) for k in zs_there]
+    planes = [[ys[dy] * 4 + xs[dx] for dx in range(4)] for dy in range(4)]
+
+    def exchange(src, dst, s_sem, r_sem):
+        for dz, dy, dx, dc in send_order():
+            zh, zl = z_parts[dz]
+            core_to = core if dc == 0 else 1 - core
+            slab_to = planes[dy][dx] * 8 + (zh * 2 + core_to)
+            send(src(slab_to, zl), dst, s_sem, r_sem, (slab_to, zl)).start()
+
+    exchange(lambda slab_to, cell_to: s1.at[pl.ds(slab_to * 2 + cell_to, 1)], r1.at[cell, pl.ds(slab, 1)], a1_s, a1_r.at[cell])
+    r1[cell, pl.ds(slab, 1), :] = s1[pl.ds(me, 1), :]
 
     tile, k2c = lax.div(me, 128), lax.rem(me, 128)
     lower = k2c < 64
@@ -449,39 +443,30 @@
 
     lax.fori_loop(0, 16, weigh, 0)
 
-    def make_profiles(slot):
-        def block(a, carry):
-            to = pl.ds(pl.multiple_of(a * 128, 128), 128)
-            for k in range(4):
-                at = slice(128 * k, 128 * k + 128)
-                high_bits = lax.shift_right_logical(cell_row_of(slot, k, 1), 7)
-                first = (high_bits == a).astype(F32).astype(BF)
-                second = (high_bits == a - 1).astype(F32).astype(BF)
-                xb[slot, to, at] = pq[slot, :, at] * first + pq[slot, :, 512 + 128 * k : 640 + 128 * k] * second
-            return carry
-
-        lax.fori_loop(0, 16, block, 0)
-
-    make_profiles(mine)
-    make_profiles(other)
-
-    @pl.when(has_prev)
-    def _():
-        for k in range(2):
-            make_profiles(2 + k)
-
     for copy in fetched[2:]:
         copy.wait()
-    whole = send(s1.at[pl.ds(0, 255)], r1.at[pl.ds(0, 255)], a1_s, a1_r, partner)
-    whole.wait_recv()
-    whole.wait_send()
-
-    high, low = zip(*(split(v) for v in decode(r1[...])))
-    whole = (jnp.concatenate(high, axis=1), jnp.concatenate(low, axis=1))
-    us[...] = dot3((cyf[0], cyf[1]), whole)
+    def half_arrived(k):
+        for count, here in ((127, cell == k), (128, cell != k)):
+
+            @pl.when(here)
+            def _(count=count):
+                send(s1.at[pl.ds(0, count)], r1.at[k, pl.ds(0, count)], a1_s, a1_r.at[k], partner).wait_recv()
+
+    def half_of(k):
+        high, low = zip(*(split(v) for v in decode(r1[k])))
+        whole = (jnp.concatenate(high, axis=1), jnp.concatenate(low, axis=1))
+        at = slice(128 * k, 128 * k + 128)
+        return dot3((cyf[0, :, at], cyf[1, :, at]), whole)
+
+    half_arrived(1)
+    us[...] = half_of(1)
+    half_arrived(0)
+    send(s1.at[pl.ds(0, 255)], s1.at[pl.ds(0, 255)], a1_s, a1_r.at[0], partner).wait_send()
+
+    us[...] += half_of(0)
 
     def y_chunk(i, carry):
-        at = pl.multiple_of(i * 16, 16)
+        at = i * 16
         c, s = ty[0, pl.ds(at, 16), :], ty[1, pl.ds(at, 16), :]
         for h in range(2):
             lanes = slice(128 * h, 128 * h + 128)
@@ -492,7 +477,8 @@
                     vs[k, pl.ds(256 * h + at, 16), 128 * half : 128 * half + 128] = parts[k]
         return carry
 
-    lax.fori_loop(0, 16, y_chunk, 0)
+    for i in range(16):
+        y_chunk(i, 0)
 
     def y_out(rows, table):
         got = dot(vs[0, rows], table)
@@ -507,7 +493,7 @@
     q_floats = [q.astype(F32) for q in qs]
 
     def scale_chunk(i, energy):
-        at = pl.multiple_of(i * 16, 16)
+        at = i * 16
         p_float = pt[pl.ds(at, 16), :]
         for h in range(2):
             value = gs[pl.ds(256 * h + at, 16), :]
@@ -520,35 +506,34 @@
                     vs[f, pl.ds(256 * h + at, 16), 128 * k : 128 * k + 128] = parts[k]
         return energy
 
-    energy = lax.fori_loop(0, 16, scale_chunk, zero8)
-
-    for f in range(2):
+    energy = zero8
+    for i in range(16):
+        energy = scale_chunk(i, energy)
+
+    def y_inverse(f):
         us[...] = dot(vs[f], bi2[f]) + dot(vs[f, :, 0:128], bi[f, 0, 1])
         for h in range(2):
             at = slice(256 * h, 256 * h + 16)
             fixed = dot3((vs[f, at, 0:128], vs[f, at, 128:256]), (bi[f, 1, 0], bi[f, 1, 1]))
             us[at, :] = jnp.where(top_row, fixed, us[at, :])
-
-        def back_chunk(i, carry, f=f):
-            at = pl.multiple_of(i * 16, 16)
-            c, s = ty[0, pl.ds(at, 16), :], ty[1, pl.ds(at, 16), :]
+        for i in range(16):
+            at = i * 16
+            c, s = ty[0, at : at + 16, :], ty[1, at : at + 16, :]
             for h in range(2):
-                re, im = us[pl.ds(256 * h + at, 16), 0:128], us[pl.ds(256 * h + at, 16), 128:256]
-                lanes = slice(256 * f + 128 * h, 256 * f + 128 * h + 128)
+                re, im = us[256 * h + at : 256 * h + at + 16, 0:128], us[256 * h + at : 256 * h + at + 16, 128:256]
                 for half, value in enumerate((re * c - im * s, re * s + im * c)):
                     parts = split(value)
                     for k in range(2):
-                        zs[k, pl.ds(256 * half + at, 16), lanes] = parts[k]
-            return carry
-
-        lax.fori_loop(0, 16, back_chunk, 0)
+                        zs[k, 256 * half + at : 256 * half + at + 16, 128 * h : 128 * h + 128] = parts[k]
+        got = dot3((cyi[0], cyi[1]), (zs[0], zs[1]))
+        s2[f] = encode(got[:, 0:128], got[:, 128:256]).reshape(2, 128, 128)
+
     for f in range(2):
-        lanes = slice(256 * f, 256 * f + 256)
-        got = dot3((cyi[0], cyi[1]), (zs[0, :, lanes], zs[1, :, lanes]))
-        s2[f] = encode(got[:, 0:128], got[:, 128:256])
-
-    exchange(rows_of, s2, r2, a2_s, a2_r)
-    r2[:, pl.ds(me, 1), :] = s2[:, pl.ds(me, 1), :]
+        y_inverse(f)
+        exchange(
+            lambda slab_to, cell_to, f=f: s2.at[f, cell_to, pl.ds(slab_to, 1)], r2.at[f, pl.ds(me, 1)], a2_s.at[f], a2_r.at[f]
+        )
+        r2[f, pl.ds(me, 1), :] = s2[f, cell, pl.ds(slab, 1), :]
 
     def total(x):
         return jnp.sum(jnp.sum(x, axis=1, keepdims=True), axis=0, keepdims=True)
@@ -560,9 +545,73 @@
     e1[plane] = row
     for i in range(1, 16):
         send(es.at[0], e1.at[plane], e_s.at[0], e_r.at[0], device_at(lax.rem(plane + i, 16), column)).start()
-    whole = send(s2.at[:, pl.ds(0, 255)], r2.at[:, pl.ds(0, 255)], a2_s, a2_r, partner)
-    whole.wait_recv()
-    whole.wait_send()
+    def push(slot, f, halves):
+        got = dot(fb[f, 0 : 256 * halves], pq[slot])
+        for k in range(4):
+            at = slice(128 * k, 128 * k + 128)
+            high_bits = lax.shift_right_logical(cell_row_of(slot, k, 1), 7)
+            force = jnp.zeros((1, 128), F32)
+            for half in range(halves):
+                kept = got[256 * half : 256 * half + 16, at]
+                for a in range(1, 16):
+                    kept = jnp.where(high_bits == a, got[256 * half + 16 * a : 256 * half + 16 * a + 16, at], kept)
+                force = force + jnp.sum(kept * yr[slot, 16 * half : 16 * half + 16, at], axis=0, keepdims=True)
+            pf[slot, f : f + 1, at] = force
+
+    def x_gather(f):
+        for t in range(2):
+            for h, value in enumerate(decode(r2[f, 128 * t : 128 * t + 128, :])):
+                parts = split(value.T)
+                for k in range(2):
+                    for j in range(4):
+                        for half in range(2):
+                            to = 256 * half + 16 * (4 * (t + 2 * h) + j)
+                            zx[to : to + 16, 128 * k : 128 * k + 128] = parts[k][32 * j + 16 * half : 32 * j + 16 * half + 16]
+
+    def x_inverse(f, out, half):
+        base = 256 * half
+        rows, first = slice(base, base + 256), slice(base, base + 16)
+        us[rows, :] = dot(zx[rows], w2[f]) + dot(zx[rows, 0:128], w[f, 0, 1])
+        us[first, :] = dot3((zx[first, 0:128], zx[first, 128:256]), (w[f, 1, 0], w[f, 1, 1]))
+        got = {}
+        for kap in range(16):
+            rows = slice(base + 16 * kap, base + 16 * kap + 16)
+            re, im = us[rows, 0:128], us[rows, 128:256]
+            if kap == 0:
+                got[0], got[16] = re, im
+            else:
+                c, s = tx[0, kap : kap + 1, :], tx[1, kap : kap + 1, :]
+                got[kap] = (re * c - im * s, re * s + im * c)
+        for a, value in enumerate(real_back(got, 16)):
+            lanes = slice(128 * a, 128 * a + 128)
+            for g in range(REGIONS):
+                out[g, 4 * half : 4 * half + 4, lanes] = value[4 * g : 4 * g + 4]
+            near = value.astype(BF)
+            fb[f, base + 16 * a : base + 16 * a + 16, 0:128] = near
+            if a:
+                fb[f, base + 16 * a - 16 : base + 16 * a, 128:256] = near
+        fb[f, base + 240 : base + 256, 128:256] = jnp.zeros((16, 128), BF)
+
+    def give_back(slot, device, sem, into):
+        return send(pf.at[slot], pr.at[into], f_s.at[sem], f_r.at[into], device)
+
+    def arrived(f):
+        whole = send(r2.at[f, pl.ds(0, 255)], r2.at[f, pl.ds(0, 255)], a2_s.at[f], a2_r.at[f], partner)
+        whole.wait_recv()
+        whole.wait_send()
+
+    arrived(0)
+    x_gather(0)
+    for half in range(2):
+        x_inverse(0, field_x, half)
+
+    @pl.when(has_prev)
+    def _():
+        for k in range(2):
+            push(2 + k, 0, 1)
+
+    push(other, 0, 2)
+    push(mine, 0, 2)
     sums_wait = send(e1.at[pl.ds(0, 15)], e1.at[pl.ds(0, 15)], e_s.at[0], e_r.at[0], partner)
     sums_wait.wait_recv()
     sums_wait.wait_send()
@@ -571,55 +620,20 @@
     e2[column] = row
     for i in range(1, 16):
         send(es.at[1], e2.at[column], e_s.at[1], e_r.at[1], device_at(plane, lax.rem(column + i, 16))).start()
-
-    for f, out in enumerate((field_x, field_y)):
-        for t in range(2):
-            for h, value in enumerate(decode(r2[f, 128 * t : 128 * t + 128, :])):
-                parts = split(value.T)
-                for k in range(2):
-                    rows = slice(128 * (t + 2 * h), 128 * (t + 2 * h) + 128)
-                    zx[rows, 128 * k : 128 * k + 128] = parts[k]
-        us[...] = dot(zx[...], w2[f]) + dot(zx[:, 0:128], w[f, 0, 1])
-        us[0:32, :] = dot3((zx[0:32, 0:128], zx[0:32, 128:256]), (w[f, 1, 0], w[f, 1, 1]))
-
-        def out_chunk(i, carry, f=f, out=out):
-            at = pl.multiple_of(i * 16, 16)
-            got = {}
-            for kap in range(16):
-                rows = pl.ds(pl.multiple_of(32 * kap + at, 16), 16)
-                re, im = us[rows, 0:128], us[rows, 128:256]
-                if kap == 0:
-                    got[0], got[16] = re, im
-                else:
-                    c, s = tx[0, kap : kap + 1, :], tx[1, kap : kap + 1, :]
-                    got[kap] = (re * c - im * s, re * s + im * c)
-            for a, value in enumerate(real_back(got, 16)):
-                lanes = slice(128 * a, 128 * a + 128)
-                out[2 * i, :, lanes] = value[0:8]
-                out[2 * i + 1, :, lanes] = value[8:16]
-                fb[pl.ds(pl.multiple_of(32 * f + at, 16), 16), lanes] = value.astype(BF)
-            return carry
-
-        lax.fori_loop(0, 2, out_chunk, 0)
-
-    def push(slot):
-        got = dot(fb[...], xb[slot])
-        for f in range(2):
-            pf[slot, f : f + 1, :] = jnp.sum(got[32 * f : 32 * f + 32, :] * yr[slot], axis=0, keepdims=True)
-
-    def give_back(slot, device, sem, into):
-        return send(pf.at[slot], pr.at[into], f_s.at[sem], f_r.at[into], device)
-
-    push(other)
+    arrived(1)
+    x_gather(1)
+    x_inverse(1, field_y, 0)
+
+    @pl.when(has_prev)
+    def _():
+        for k in range(2):
+            push(2 + k, 1, 1)
+            give_back(2 + k, (slab - 1, k), 1 + k, 1).start()
+
+    x_inverse(1, field_y, 1)
+    push(other, 1, 2)
     give_back(other, partner, 0, 0).start()
-
-    @pl.when(has_prev)
-    def _():
-        for k in range(2):
-            push(2 + k)
-            give_back(2 + k, (slab - 1, k), 1 + k, 1).start()
-
-    push(mine)
+    push(mine, 1, 2)
 
     @pl.when(jnp.logical_not(has_next))
     def _():
@@ -651,16 +665,14 @@
             copy.wait_send()
 
 
-def finish(field_x, field_y, force, sums, out_x, out_y, out_force, energy, overflow, sem):
-    copies = [
-        pltpu.make_async_copy(src, dst, sem.at[k])
-        for k, (src, dst) in enumerate(((field_x, out_x), (field_y, out_y), (force, out_force)))
-    ]
+def finish(field_x, field_y, force, sums, out_x, out_y, out_force, energy, overflow, small, sem):
+    row = sums[...]
+    small[0] = row[:, 2:3]
+    small[1] = row[:, 0:1] / row[:, 1:2]
+    pairs = ((field_x, out_x), (field_y, out_y), (force, out_force), (small.at[0], energy), (small.at[1], overflow))
+    copies = [pltpu.make_async_copy(src, dst, sem.at[k]) for k, (src, dst) in enumerate(pairs)]
     for copy in copies:
         copy.start()
-    row = sums[...]
-    energy[...] = row[:, 2:3]
-    overflow[...] = row[:, 0:1] / row[:, 1:2]
     for copy in copies:
         copy.wait()
 
@@ -675,23 +687,22 @@
     scratch = [
         V((4, 5, 4, 128), I32),
         V((4, 2, CELLS_DEV), F32),
-        V((4, 128, 1024), BF),
-        V((512, 1024), BF),
+        V((4, 256, 512), BF),
+        V((2, 512, 512), BF),
         V((4, 32, CELLS_DEV), F32),
-        V((4, M, CELLS_DEV), BF),
-        V((512, 128), F32),
-        V((2, 512, 512), BF),
+        V((512, 256), F32),
+        V((2, 512, 256), BF),
         V((256, 128), I32),
-        V((256, 128), I32),
+        V((2, 128, 128), I32),
         V((512, 256), F32),
         V((2, 512, 256), BF),
         V((512, 128), F32),
         V((512, 128), F32),
         V((256, 128), F32),
-        V((2, 256, 128), I32),
+        V((2, 2, 128, 128), I32),
         V((2, 256, 128), I32),
         V((512, 256), BF),
-        V((64, M), BF),
+        V((2, 512, 256), BF),
         V((4, 2, CELLS_DEV), F32),
         V((2, 2, CELLS_DEV), F32),
         V((16, 1, 128), F32),
@@ -709,7 +720,7 @@
         D((11,)), D((6,)),
         pltpu.SemaphoreType.REGULAR,
         D((4,)), D((2, 4)),
-        D, D, D, D,
+        D, D((2,)), D((2,)), D((2,)),
         D((3,)), D((2,)),
         D((2,)), D((2,)),
     ]
@@ -730,8 +741,8 @@
         finish,
         out_shape=(S(field, F32), S(field, F32), S((2, CELLS_DEV), F32), S((1, 1), F32), S((1, 1), F32)),
         in_specs=[vmem] * 4,
-        out_specs=(hbm, hbm, hbm, vmem, vmem),
-        scratch_shapes=[D((3,))],
+        out_specs=(hbm,) * 5,
+        scratch_shapes=[V((2, 1, 1), F32), D((5,))],
         compiler_params=pltpu.CompilerParams(vmem_limit_bytes=4 * 1024 * 1024),
         name="finish",
     )(*results)

time: 46.2 us -> 41.6 us (0.900)
  Pallas kernels: 45.5 us -> 40.9 us
    pallas_call x1, Pallas kernels: 44.1 us -> 40.1 us  [body(): pl.pallas_call(kernel, out_shape=(V(field, F32), V(field, F32), V((2, CEL...]
    pallas_call x1, Pallas kernels: 1.33 us -> 0.84 us  [body(): pl.pallas_call(finish, out_shape=(S(field, F32), S(field, F32), S((2, CEL...]
where the time goes in v3:
time: 41.6 us; the launch traced here: 41.5 us
  Pallas kernels  40.9 us (98%)
  between operations  0.64 us (2%)
    pallas_call x1, Pallas kernels, body(): pl.pallas_call(kernel, out_shape=(V(field, F32), V(field, F32), V((2, CEL...  40.1 us
    pallas_call x1, Pallas kernels, body(): pl.pallas_call(finish, out_shape=(S(field, F32), S(field, F32), S((2, CEL...  0.84 us

profile of v3, /device:TPU:1, one launch (start us, length us, event | category | flops | bytes accessed | tf_op | source)
XLA Modules:
  0.0 41.5 jit_solution(8049757705606040275)
XLA Ops:
  0.6 40.1 %placement.1 = (f32[4,8,2048]{2,1,0:T(8,128)S(1)}, f32[4,8,2048]{2,1,0:T(8,128)S(1)}, f32[2,512]{1,0:T(2,128)S(1)}, f32[1,128]{1,0:T(1,128)S(1)}) custom-call(s32[4,128]{1,0:T(4,128)} %bitcast.7, s32[4,128]{1,0:T(4,128)} %bitcast.8, s32[4,128]{1,0:T(4,128)} %bitcast.9, s32[4,128]{1,0:T(4,128)} %bitcast.10, s32[4,128]{1,0:T(4,128)} %bitcast.11, ...), custom_call_target="tpu_custom_call" | custom-call | tf_op jit(solution)/shard_map/placement/pallas_call | solution.py:728
  40.7 0.8 %finish.1 = (f32[4,8,2048]{2,1,0:T(8,128)}, f32[4,8,2048]{2,1,0:T(8,128)}, f32[2,512]{1,0:T(2,128)}, f32[1,1]{1,0:T(1,128)}, f32[1,1]{1,0:T(1,128)}) custom-call(f32[4,8,2048]{2,1,0:T(8,128)S(1)} %get-tuple-element.14.field_x, f32[4,8,2048]{2,1,0:T(8,128)S(1)} %get-tuple-element.15.field_y, f32[2,512]{1,0:T(2,128)S(1)} %get-tuple-element.16.force, ...), custom_call_target="tpu_custom_call" | custom-call | tf_op jit(solution)/shard_map/finish/pallas_call | solution.py:740

commit v4 on v3

--- a/solution.py
+++ b/solution.py
@@ -18,6 +18,8 @@
 I32 = jnp.int32
 MESH = pl.DeviceIdType.MESH
 STEP = math.pi / M
+FAR = 98
+NEXT = 14
 
 
 def c_add(x,y): return (x[0]+y[0], x[1]+y[1])
@@ -213,6 +215,10 @@
     return sorted(every, key=lambda d: (-hops[d], rng.random()))
 
 
+def in_two(count, base=0):
+    return [slice(base + k * count // 2, base + (k + 1) * count // 2) for k in range(2)]
+
+
 def place():
     slab = lax.axis_index("slab")
     cell = lax.axis_index("cell")
@@ -231,7 +237,7 @@
     row_h, col_h, width_h, height_h, region_h, offset_h,
     w_h, tx_h, cyf_h, cyi_h, ty_h, bf_h, bi_h,
     field_x, field_y, force, sums,
-    ci, co, pq, ym, yr, d2, zs, s1, r1, us, vs, gs, aw, pt, s2, r2, zx, fb, pf, pr, e1, e2, es,
+    ci, co, pq, ym, yr, d2, zs, s1, r1, us, vs, tops, gs, aw, pt, s2, r2, zx, fb, pf, pr, e1, e2, es,
     w, w2, tx, cyf, cyi, ty, bf, bi, bi2,
     const_sem, in_sem, met, cell_s, cell_r, a1_s, a1_r, a2_s, a2_r, f_s, f_r, e_s, e_r,
 ):
@@ -253,6 +259,11 @@
     def signal_at(sem, device):
         pl.semaphore_signal(sem, inc=1, device_id=device, device_id_type=MESH)
 
+    plane_peers = [device_at(lax.rem(plane + i, 16), column) for i in (10, 6, 9, 11, 5, 7, 8, 2, 14, 13, 3, 4, 12, 1, 15)]
+    column_peers = [device_at(plane, lax.rem(column + i, 16)) for i in (8, 7, 9, 6, 10, 5, 11, 4, 12, 3, 13, 2, 14, 1, 15)]
+    for device in plane_peers + column_peers:
+        signal_at(barrier, device)
+
     @pl.when(has_prev)
     def _():
         signal_at(barrier, (slab - 1, 0))
@@ -263,23 +274,6 @@
     ys = [lax.rem(py + k, 4) for k in range(4)]
     xs = [lax.rem(px + k, 4) for k in range(4)]
 
-    plane_peers = [device_at(lax.rem(plane + i, 16), column) for i in range(1, 16)]
-    column_peers = [device_at(plane, lax.rem(column + i, 16)) for i in range(1, 16)]
-    for device in plane_peers + column_peers:
-        signal_at(barrier, device)
-
-    fetched = [
-        pltpu.make_async_copy(src, dst, const_sem.at[k])
-        for k, (src, dst) in enumerate(
-            (
-                (tx_h, tx), (w_h, w), (w_h.at[:, 0, 0], w2.at[:, 0:128]), (w_h.at[:, 0, 0], w2.at[:, 128:256]),
-                (cyf_h, cyf), (ty_h, ty), (bf_h, bf), (bi_h, bi),
-                (bi_h.at[:, 0, 0], bi2.at[:, 0:128]), (bi_h.at[:, 0, 0], bi2.at[:, 128:256]), (cyi_h, cyi),
-            )
-        )
-    ]
-    for copy in fetched:
-        copy.start()
     for copy in own:
         copy.wait()
 
@@ -340,15 +334,30 @@
     for device in column_peers:
         signal_at(met, device)
 
+    fetched = [
+        pltpu.make_async_copy(src, dst, const_sem.at[k])
+        for k, (src, dst) in enumerate(
+            (
+                (tx_h, tx), (w_h, w), (w_h.at[:, 0, 0], w2.at[:, 0:128]), (w_h.at[:, 0, 0], w2.at[:, 128:256]),
+                (cyf_h, cyf), (ty_h, ty), (bf_h, bf), (bi_h, bi),
+                (bi_h.at[:, 0, 0], bi2.at[:, 0:128]), (bi_h.at[:, 0, 0], bi2.at[:, 128:256]), (cyi_h, cyi),
+            )
+        )
+    ]
+    for copy in fetched:
+        copy.start()
+
     def arrive(slot):
         send(ci.at[slot], ci.at[slot], cell_s.at[0], cell_r.at[0, slot], partner).wait_recv()
         send(co.at[slot], co.at[slot], cell_s.at[1], cell_r.at[1, slot], partner).wait_recv()
 
     make_cells(mine, 2, ym.at[0])
-    d2[...] = dot_nt(ym[0], pq[mine])
+    for rows in in_two(512):
+        d2[rows] = dot_nt(ym[0, rows], pq[mine])
     arrive(other)
     make_cells(other, 2, ym.at[0])
-    d2[...] += dot_nt(ym[0], pq[other])
+    for rows in in_two(512):
+        d2[rows] += dot_nt(ym[0, rows], pq[other])
 
     @pl.when(has_prev)
     def _():
@@ -397,15 +406,14 @@
         s1[128 * t : 128 * t + 128, :] = encode(tiles[t], tiles[t + 2])
 
     pl.semaphore_wait(met, 15)
-    zs_there = [lax.rem(z + k, 8) for k in range(8)]
-    z_parts = [(lax.div(k, 2), lax.rem(k, 2)) for k in zs_there]
     planes = [[ys[dy] * 4 + xs[dx] for dx in range(4)] for dy in range(4)]
-
-    def exchange(src, dst, s_sem, r_sem):
-        for dz, dy, dx, dc in send_order():
+    z_there = [lax.rem(z + k, 8) for k in range(8)]
+    z_parts = [(lax.div(k, 2), lax.rem(k, 2)) for k in z_there]
+
+    def exchange(src, dst, s_sem, r_sem, part=slice(None)):
+        for dz, dy, dx, dc in send_order()[part]:
             zh, zl = z_parts[dz]
-            core_to = core if dc == 0 else 1 - core
-            slab_to = planes[dy][dx] * 8 + (zh * 2 + core_to)
+            slab_to = planes[dy][dx] * 8 + (zh * 2 + (core if dc == 0 else 1 - core))
             send(src(slab_to, zl), dst, s_sem, r_sem, (slab_to, zl)).start()
 
     exchange(lambda slab_to, cell_to: s1.at[pl.ds(slab_to * 2 + cell_to, 1)], r1.at[cell, pl.ds(slab, 1)], a1_s, a1_r.at[cell])
@@ -456,14 +464,16 @@
         high, low = zip(*(split(v) for v in decode(r1[k])))
         whole = (jnp.concatenate(high, axis=1), jnp.concatenate(low, axis=1))
         at = slice(128 * k, 128 * k + 128)
-        return dot3((cyf[0, :, at], cyf[1, :, at]), whole)
+        return [(rows, dot3((cyf[0, rows, at], cyf[1, rows, at]), whole)) for rows in in_two(512)]
 
     half_arrived(1)
-    us[...] = half_of(1)
+    for rows, got in half_of(1):
+        us[rows] = got
     half_arrived(0)
     send(s1.at[pl.ds(0, 255)], s1.at[pl.ds(0, 255)], a1_s, a1_r.at[0], partner).wait_send()
 
-    us[...] += half_of(0)
+    for rows, got in half_of(0):
+        us[rows] += got
 
     def y_chunk(i, carry):
         at = i * 16
@@ -484,7 +494,8 @@
         got = dot(vs[0, rows], table)
         return got[:, 0:128] + (got[:, 128:256] + dot(vs[1, rows], table[:, 0:128]))
 
-    gs[...] = y_out(slice(0, 512), bf[0])
+    for rows in in_two(512):
+        gs[rows] = y_out(rows, bf[0])
     top_row = lax.broadcasted_iota(I32, (16, 1), 0) == 0
     for h in range(2):
         at = slice(256 * h, 256 * h + 16)
@@ -510,30 +521,62 @@
     for i in range(16):
         energy = scale_chunk(i, energy)
 
-    def y_inverse(f):
-        us[...] = dot(vs[f], bi2[f]) + dot(vs[f, :, 0:128], bi[f, 0, 1])
+    def top_rows(f, h):
+        at = slice(256 * h, 256 * h + 16)
+        return dot3((vs[f, at, 0:128], vs[f, at, 128:256]), (bi[f, 1, 0], bi[f, 1, 1]))
+
+    def turned(values, c, s):
+        re, im = values[:, 0:128], values[:, 128:256]
+        return [split(value) for value in (re * c - im * s, re * s + im * c)]
+
+    def keep_turned(values, h, at):
+        for half in range(2):
+            for k in range(2):
+                zs[k, pl.ds(256 * half + at, values[half][k].shape[0]), 128 * h : 128 * h + 128] = values[half][k]
+
+    def copies_of(f):
+        return (
+            lambda slab_to, cell_to: s2.at[f, cell_to, pl.ds(slab_to, 1)], r2.at[f, pl.ds(me, 1)], a2_s.at[f], a2_r.at[f]
+        )
+
+    for rows in in_two(512):
+        us[rows] = dot(vs[0, rows], bi2[0]) + dot(vs[0, rows, 0:128], bi[0, 0, 1])
+    for h in range(2):
+        at = slice(256 * h, 256 * h + 16)
+        us[at, :] = jnp.where(top_row, top_rows(0, h), us[at, :])
+        tops[h] = top_rows(1, h)
+    for i in range(16):
         for h in range(2):
-            at = slice(256 * h, 256 * h + 16)
-            fixed = dot3((vs[f, at, 0:128], vs[f, at, 128:256]), (bi[f, 1, 0], bi[f, 1, 1]))
-            us[at, :] = jnp.where(top_row, fixed, us[at, :])
-        for i in range(16):
-            at = i * 16
-            c, s = ty[0, at : at + 16, :], ty[1, at : at + 16, :]
-            for h in range(2):
-                re, im = us[256 * h + at : 256 * h + at + 16, 0:128], us[256 * h + at : 256 * h + at + 16, 128:256]
-                for half, value in enumerate((re * c - im * s, re * s + im * c)):
-                    parts = split(value)
-                    for k in range(2):
-                        zs[k, 256 * half + at : 256 * half + at + 16, 128 * h : 128 * h + 128] = parts[k]
-        got = dot3((cyi[0], cyi[1]), (zs[0], zs[1]))
-        s2[f] = encode(got[:, 0:128], got[:, 128:256]).reshape(2, 128, 128)
-
-    for f in range(2):
-        y_inverse(f)
-        exchange(
-            lambda slab_to, cell_to, f=f: s2.at[f, cell_to, pl.ds(slab_to, 1)], r2.at[f, pl.ds(me, 1)], a2_s.at[f], a2_r.at[f]
-        )
-        r2[f, pl.ds(me, 1), :] = s2[f, cell, pl.ds(slab, 1), :]
+            at = slice(16 * i, 16 * i + 16)
+            keep_turned(turned(us[256 * h + 16 * i : 256 * h + 16 * i + 16, :], ty[0, at, :], ty[1, at, :]), h, 16 * i)
+    for k, rows in enumerate(in_two(256)):
+        got = dot3((cyi[0, rows], cyi[1, rows]), (zs[0], zs[1]))
+        s2[0, k] = encode(got[:, 0:128], got[:, 128:256])
+    r2[0, pl.ds(me, 1), :] = s2[0, cell, pl.ds(slab, 1), :]
+
+    for i in range(2):
+        at = 128 * i
+        rows = [vs[1, 256 * h + at : 256 * h + at + 128, :] for h in range(2)]
+        c, s = ty[0, at : at + 128, :], ty[1, at : at + 128, :]
+        top = [tops[h] for h in range(2)]
+        got = [dot(r, bi2[1]) + dot(r[:, 0:128], bi[1, 0, 1]) for r in rows]
+        values = []
+        for h in range(2):
+            value = got[h]
+            if i == 0:
+                value = jnp.concatenate([jnp.where(top_row, top[h], value[0:16]), value[16:]], axis=0)
+            values.append(turned(value, c, s))
+        exchange(*copies_of(0), part=slice(FAR // 2 * i, FAR // 2 * i + FAR // 2))
+        for h in range(2):
+            keep_turned(values[h], h, at)
+
+    for k, rows in enumerate(in_two(256)):
+        got = dot3((cyi[0, rows], cyi[1, rows]), (zs[0], zs[1]))
+        s2[1, k] = encode(got[:, 0:128], got[:, 128:256])
+    exchange(*copies_of(1), part=slice(0, NEXT))
+    exchange(*copies_of(0), part=slice(FAR, None))
+    exchange(*copies_of(1), part=slice(NEXT, None))
+    r2[1, pl.ds(me, 1), :] = s2[1, cell, pl.ds(slab, 1), :]
 
     def total(x):
         return jnp.sum(jnp.sum(x, axis=1, keepdims=True), axis=0, keepdims=True)
@@ -568,11 +611,16 @@
                             to = 256 * half + 16 * (4 * (t + 2 * h) + j)
                             zx[to : to + 16, 128 * k : 128 * k + 128] = parts[k][32 * j + 16 * half : 32 * j + 16 * half + 16]
 
+    def x_product(f, halves):
+        base, count = 256 * halves[0], 256 * len(halves)
+        for rows in in_two(count, base):
+            us[rows, :] = dot(zx[rows], w2[f]) + dot(zx[rows, 0:128], w[f, 0, 1])
+        for half in halves:
+            first = slice(256 * half, 256 * half + 16)
+            us[first, :] = dot3((zx[first, 0:128], zx[first, 128:256]), (w[f, 1, 0], w[f, 1, 1]))
+
     def x_inverse(f, out, half):
         base = 256 * half
-        rows, first = slice(base, base + 256), slice(base, base + 16)
-        us[rows, :] = dot(zx[rows], w2[f]) + dot(zx[rows, 0:128], w[f, 0, 1])
-        us[first, :] = dot3((zx[first, 0:128], zx[first, 128:256]), (w[f, 1, 0], w[f, 1, 1]))
         got = {}
         for kap in range(16):
             rows = slice(base + 16 * kap, base + 16 * kap + 16)
@@ -602,6 +650,7 @@
 
     arrived(0)
     x_gather(0)
+    x_product(0, (0, 1))
     for half in range(2):
         x_inverse(0, field_x, half)
 
@@ -622,14 +671,17 @@
         send(es.at[1], e2.at[column], e_s.at[1], e_r.at[1], device_at(plane, lax.rem(column + i, 16))).start()
     arrived(1)
     x_gather(1)
+    x_product(1, (0,))
     x_inverse(1, field_y, 0)
 
     @pl.when(has_prev)
     def _():
         for k in range(2):
             push(2 + k, 1, 1)
+        for k in range(2):
             give_back(2 + k, (slab - 1, k), 1 + k, 1).start()
 
+    x_product(1, (1,))
     x_inverse(1, field_y, 1)
     push(other, 1, 2)
     give_back(other, partner, 0, 0).start()
@@ -696,6 +748,7 @@
         V((2, 128, 128), I32),
         V((512, 256), F32),
         V((2, 512, 256), BF),
+        V((2, 16, 256), F32),
         V((512, 128), F32),
         V((512, 128), F32),
         V((256, 128), F32),

time: 41.6 us -> 40.7 us (0.978)
  Pallas kernels: 40.9 us -> 40 us
    pallas_call x1, Pallas kernels: 40.1 us -> 39.1 us  [body(): pl.pallas_call(kernel, out_shape=(V(field, F32), V(field, F32), V((2, CEL...]
where the time goes in v4:
time: 40.7 us; the launch traced here: 40.6 us
  Pallas kernels  40 us (98%)
  between operations  0.64 us (2%)
    pallas_call x1, Pallas kernels, body(): pl.pallas_call(kernel, out_shape=(V(field, F32), V(field, F32), V((2, CEL...  39.1 us
    pallas_call x1, Pallas kernels, body(): pl.pallas_call(finish, out_shape=(S(field, F32), S(field, F32), S((2, CEL...  0.84 us

profile of v4, /device:TPU:1, one launch (start us, length us, event | category | flops | bytes accessed | tf_op | source)
XLA Modules:
  0.0 40.6 jit_solution(1214507530709230589)
XLA Ops:
  0.6 39.1 %placement.1 = (f32[4,8,2048]{2,1,0:T(8,128)S(1)}, f32[4,8,2048]{2,1,0:T(8,128)S(1)}, f32[2,512]{1,0:T(2,128)S(1)}, f32[1,128]{1,0:T(1,128)S(1)}) custom-call(s32[4,128]{1,0:T(4,128)} %bitcast.7, s32[4,128]{1,0:T(4,128)} %bitcast.8, s32[4,128]{1,0:T(4,128)} %bitcast.9, s32[4,128]{1,0:T(4,128)} %bitcast.10, s32[4,128]{1,0:T(4,128)} %bitcast.11, ...), custom_call_target="tpu_custom_call" | custom-call | tf_op jit(solution)/shard_map/placement/pallas_call | solution.py:781
  39.8 0.8 %finish.1 = (f32[4,8,2048]{2,1,0:T(8,128)}, f32[4,8,2048]{2,1,0:T(8,128)}, f32[2,512]{1,0:T(2,128)}, f32[1,1]{1,0:T(1,128)}, f32[1,1]{1,0:T(1,128)}) custom-call(f32[4,8,2048]{2,1,0:T(8,128)S(1)} %get-tuple-element.14.field_x, f32[4,8,2048]{2,1,0:T(8,128)S(1)} %get-tuple-element.15.field_y, f32[2,512]{1,0:T(2,128)S(1)} %get-tuple-element.16.force, ...), custom_call_target="tpu_custom_call" | custom-call | tf_op jit(solution)/shard_map/finish/pallas_call | solution.py:793

commit v5 on v4

--- a/solution.py
+++ b/solution.py
@@ -135,6 +135,7 @@
     ws = np.block([[s1, -c1], [s2, c2]])
     ws0 = np.block([[s1, zero], [zero, sm]])
     w = np.stack([split_np(m) for m in (ws, ws0, wc, wc0)]).reshape(2, 2, 2, 128, 256)
+    wt = np.stack([np.concatenate(list(split_np(m.T)), axis=1) for m in (wc, wc0)])
     kap = np.arange(16)[:, None]
     ang = pi * kap * (2 * b + 1) / 4096
     tx = np.stack([np.cos(ang), np.sin(ang)]).astype(np.float32)
@@ -144,7 +145,7 @@
     cim[0] = (-1.0) ** np.arange(256)
     cy = np.concatenate([cre, cim], 0)[:, np.arange(256).reshape(128, 2).T.reshape(-1)]
     ours = np.arange(128).reshape(4, 4, 2, 4).transpose(0, 2, 1, 3).reshape(-1)
-    cy_fwd, cy_inv = split_np(cy), split_np(cy.T)
+    cy_fwd = split_np(cy)
     r = np.arange(8)
     angy = pi * p1 * (2 * r[None, :] + 1) / 4096
     ty = np.stack([np.tile(np.cos(angy), (1, 16)), np.tile(np.sin(angy), (1, 16))])[:, :, ours].astype(np.float32)
@@ -163,7 +164,7 @@
 
     b_fwd = np.stack([np.concatenate(list(split_np(wide(m))), axis=1) for m in (bc, bc0)])
     b_inv = np.stack([split_np(wide(m).T) for m in (bc, bc0, bs, bs0)]).reshape(2, 2, 2, 128, 256)
-    return w, tx, cy_fwd, cy_inv, ty, b_fwd, b_inv
+    return w, wt, tx, cy_fwd, ty, b_fwd, b_inv
 
 
 def dot(x, y):
@@ -235,10 +236,10 @@
 
 def kernel(
     row_h, col_h, width_h, height_h, region_h, offset_h,
-    w_h, tx_h, cyf_h, cyi_h, ty_h, bf_h, bi_h,
+    w_h, wt_h, tx_h, cyf_h, ty_h, bf_h, bi_h,
     field_x, field_y, force, sums,
-    ci, co, pq, ym, yr, d2, zs, s1, r1, us, vs, tops, gs, aw, pt, s2, r2, zx, fb, pf, pr, e1, e2, es,
-    w, w2, tx, cyf, cyi, ty, bf, bi, bi2,
+    ci, co, pq, ym, yr, d2, zs, s1, r1, us, vs, gs, aw, pt, s2, r2, zx, fb, pf, pr, e1, e2, es,
+    w, w2, wt, tx, cyf, cyi, ty, bf, bi, bi2,
     const_sem, in_sem, met, cell_s, cell_r, a1_s, a1_r, a2_s, a2_r, f_s, f_r, e_s, e_r,
 ):
     slab, cell, plane, column = place()
@@ -259,9 +260,13 @@
     def signal_at(sem, device):
         pl.semaphore_signal(sem, inc=1, device_id=device, device_id_type=MESH)
 
-    plane_peers = [device_at(lax.rem(plane + i, 16), column) for i in (10, 6, 9, 11, 5, 7, 8, 2, 14, 13, 3, 4, 12, 1, 15)]
+    py, px = lax.div(plane, 4), lax.rem(plane, 4)
+    ys = [lax.rem(py + k, 4) for k in range(4)]
+    xs = [lax.rem(px + k, 4) for k in range(4)]
+    x_line = [device_at(py * 4 + xs[k], column) for k in (2, 1, 3)]
+    y_line = [device_at(ys[k] * 4 + px, column) for k in (2, 1, 3)]
     column_peers = [device_at(plane, lax.rem(column + i, 16)) for i in (8, 7, 9, 6, 10, 5, 11, 4, 12, 3, 13, 2, 14, 1, 15)]
-    for device in plane_peers + column_peers:
+    for device in column_peers + x_line + y_line:
         signal_at(barrier, device)
 
     @pl.when(has_prev)
@@ -269,10 +274,7 @@
         signal_at(barrier, (slab - 1, 0))
         signal_at(barrier, (slab - 1, 1))
 
-    py, px = lax.div(plane, 4), lax.rem(plane, 4)
     z, core = lax.div(column, 4) * 2 + cell, lax.rem(lax.div(column, 2), 2)
-    ys = [lax.rem(py + k, 4) for k in range(4)]
-    xs = [lax.rem(px + k, 4) for k in range(4)]
 
     for copy in own:
         copy.wait()
@@ -283,7 +285,7 @@
         return ci[slot, which, k : k + 1, :]
 
     def make_cells(slot, halves, masked):
-        bins = lax.broadcasted_iota(I32, (128, 128), 0).astype(F32)
+        bins = lax.broadcasted_iota(I32, (128, 128), 0).astype(F32).astype(BF)
         line = lax.broadcasted_iota(I32, (16, 128), 0)
         rows = (jnp.bitwise_and(line, 3) + low_row).astype(F32)
         region_of = lax.shift_right_logical(line, 2)
@@ -291,12 +293,18 @@
             at = slice(128 * k, 128 * k + 128)
             col = cell_row_of(slot, k, 1)
             high_bits = lax.shift_right_logical(col, 7)
-            low_bits = (col - high_bits * 128).astype(F32)
+            low_bits = (col - high_bits * 128).astype(F32).astype(BF)
             start = co[slot, 0:1, at]
-            end = start + cell_row_of(slot, k, 2).astype(F32)
+            width = cell_row_of(slot, k, 2).astype(F32)
+            first = (1.0 - start).astype(BF)
+            last = ((start + width) - width).astype(BF)
+            width = width.astype(BF)
             reach = bins - low_bits
-            pq[slot, 0:128, at] = overlap(reach, start, end).astype(BF)
-            pq[slot, 128:256, at] = overlap(reach + 128.0, start, end).astype(BF)
+            for far in range(2):
+                if far:
+                    reach = reach + BF(128.0)
+                got = jnp.minimum(reach + first, (width - reach) + last)
+                pq[slot, 128 * far : 128 * far + 128, at] = jnp.clip(got, BF(0.0), BF(1.0))
             start = co[slot, 1:2, at]
             end = start + cell_row_of(slot, k, 3).astype(F32)
             reach = rows - cell_row_of(slot, k, 0).astype(F32)
@@ -313,7 +321,7 @@
             src_ref=src, dst_ref=dst, send_sem=s_sem, recv_sem=r_sem, device_id=device, device_id_type=MESH
         )
 
-    pl.semaphore_wait(barrier, 30 + has_next.astype(I32))
+    pl.semaphore_wait(barrier, 21 + has_next.astype(I32))
     partner = (slab, other)
     give = [
         send(ci.at[mine], ci.at[mine], cell_s.at[0], cell_r.at[0, mine], partner),
@@ -331,16 +339,16 @@
         for copy in give_next:
             copy.start()
 
-    for device in column_peers:
-        signal_at(met, device)
+    for device in x_line:
+        signal_at(met.at[0], device)
 
     fetched = [
         pltpu.make_async_copy(src, dst, const_sem.at[k])
         for k, (src, dst) in enumerate(
             (
-                (tx_h, tx), (w_h, w), (w_h.at[:, 0, 0], w2.at[:, 0:128]), (w_h.at[:, 0, 0], w2.at[:, 128:256]),
+                (tx_h, tx), (wt_h, wt), (w_h, w), (w_h.at[:, 0, 0], w2.at[:, 0:128]), (w_h.at[:, 0, 0], w2.at[:, 128:256]),
                 (cyf_h, cyf), (ty_h, ty), (bf_h, bf), (bi_h, bi),
-                (bi_h.at[:, 0, 0], bi2.at[:, 0:128]), (bi_h.at[:, 0, 0], bi2.at[:, 128:256]), (cyi_h, cyi),
+                (bi_h.at[:, 0, 0], bi2.at[:, 0:128]), (bi_h.at[:, 0, 0], bi2.at[:, 128:256]),
             )
         )
     ]
@@ -355,28 +363,21 @@
     for rows in in_two(512):
         d2[rows] = dot_nt(ym[0, rows], pq[mine])
     arrive(other)
+    pl.semaphore_wait(met.at[0], 3)
+    for device in y_line:
+        signal_at(met.at[1], device)
     make_cells(other, 2, ym.at[0])
     for rows in in_two(512):
         d2[rows] += dot_nt(ym[0, rows], pq[other])
 
-    @pl.when(has_prev)
-    def _():
-        for k in range(2):
-            arrive(2 + k)
-            make_cells(2 + k, 1, ym.at[k])
-        d2[0:256, :] += dot_nt(ym[0, 0:256], pq[2]) + dot_nt(ym[1, 0:256], pq[3])
-
     zero8 = jnp.zeros((8, 128), F32)
     lane = lax.broadcasted_iota(I32, (1, 128), 1)
     first_group = lane < 32
 
-    fetched[0].wait()
-
-    excess = area = zero8
-    for i in range(2):
+    def x_forward(half, excess, area):
         here = []
         for a in range(16):
-            at = 256 * i + 16 * a
+            at = 256 * half + 16 * a
             value = d2[at : at + 16, 0:128]
             if a:
                 value = value + d2[at - 16 : at, 128:256]
@@ -386,26 +387,49 @@
             area = area + (value[0:8] + value[8:16])
         got = real_spectrum(here)
         for kap in range(16):
-            at = slice(32 * kap + 16 * i, 32 * kap + 16 * i + 16)
+            at = slice(256 * half + 16 * kap, 256 * half + 16 * kap + 16)
             if kap == 0:
                 pair = (got[0], got[16])
             else:
                 (re, im), c, s = got[kap], tx[0, kap : kap + 1, :], tx[1, kap : kap + 1, :]
                 pair = (re * c + im * s, im * c - re * s)
-            for half, value in enumerate(pair):
+            for part, value in enumerate(pair):
                 parts = split(value)
                 for k in range(2):
-                    zs[k, at, 128 * half : 128 * half + 128] = parts[k]
+                    zs[k, at, 128 * part : 128 * part + 128] = parts[k]
+
+        def product(rows, kind):
+            got = dot(zs[0, rows], wt[kind])
+            return got[:, 0:128] + (got[:, 128:256] + dot(zs[1, rows], wt[kind, :, 0:128]))
+
+        for rows in in_two(256, 256 * half):
+            gs[rows] = product(rows, 0)
+        first = slice(256 * half, 256 * half + 16)
+        gs[first] = product(first, 1)
+        return excess, area
+
+    fetched[0].wait()
     fetched[1].wait()
-    table, first = (w[1, 0, 0], w[1, 0, 1]), (w[1, 1, 0], w[1, 1, 1])
-    got = dot3_nt(table, (zs[0], zs[1]))
-    fixed = dot3_nt(first, (zs[0, 0:128], zs[1, 0:128]))
-    tiles = [got[:, 128 * t : 128 * t + 128] for t in range(4)]
-    tiles[0] = jnp.where(first_group, fixed, tiles[0])
+    excess, area = x_forward(1, zero8, zero8)
+
+    @pl.when(has_prev)
+    def _():
+        for k in range(2):
+            arrive(2 + k)
+        for k in range(2):
+            make_cells(2 + k, 1, ym.at[1 + k])
+        for rows in in_two(256):
+            d2[rows] += dot_nt(ym[1, rows], pq[2]) + dot_nt(ym[2, rows], pq[3])
+
+    excess, area = x_forward(0, excess, area)
+    tiles = []
+    for t in range(4):
+        rows = [gs[256 * half + 16 * kap : 256 * half + 16 * kap + 16] for kap in range(4 * t, 4 * t + 4) for half in range(2)]
+        tiles.append(jnp.concatenate(rows, axis=0).T)
     for t in range(2):
         s1[128 * t : 128 * t + 128, :] = encode(tiles[t], tiles[t + 2])
 
-    pl.semaphore_wait(met, 15)
+    pl.semaphore_wait(met.at[1], 3)
     planes = [[ys[dy] * 4 + xs[dx] for dx in range(4)] for dy in range(4)]
     z_there = [lax.rem(z + k, 8) for k in range(8)]
     z_parts = [(lax.div(k, 2), lax.rem(k, 2)) for k in z_there]
@@ -453,6 +477,11 @@
 
     for copy in fetched[2:]:
         copy.wait()
+    for k in range(2):
+        for i in range(4):
+            for j in range(2):
+                rows, lanes = slice(128 * i, 128 * i + 128), slice(128 * j, 128 * j + 128)
+                cyi[k, lanes, rows] = cyf[k, rows, lanes].T
     def half_arrived(k):
         for count, here in ((127, cell == k), (128, cell != k)):
 
@@ -544,21 +573,23 @@
     for h in range(2):
         at = slice(256 * h, 256 * h + 16)
         us[at, :] = jnp.where(top_row, top_rows(0, h), us[at, :])
-        tops[h] = top_rows(1, h)
     for i in range(16):
         for h in range(2):
             at = slice(16 * i, 16 * i + 16)
             keep_turned(turned(us[256 * h + 16 * i : 256 * h + 16 * i + 16, :], ty[0, at, :], ty[1, at, :]), h, 16 * i)
-    for k, rows in enumerate(in_two(256)):
-        got = dot3((cyi[0, rows], cyi[1, rows]), (zs[0], zs[1]))
-        s2[0, k] = encode(got[:, 0:128], got[:, 128:256])
+    def back_in_y(f):
+        for k, rows in enumerate(in_two(256)):
+            got = dot3((cyi[0, rows], cyi[1, rows]), (zs[0], zs[1]))
+            s2[f, k] = encode(got[:, 0:128], got[:, 128:256])
+
+    back_in_y(0)
     r2[0, pl.ds(me, 1), :] = s2[0, cell, pl.ds(slab, 1), :]
 
     for i in range(2):
         at = 128 * i
         rows = [vs[1, 256 * h + at : 256 * h + at + 128, :] for h in range(2)]
         c, s = ty[0, at : at + 128, :], ty[1, at : at + 128, :]
-        top = [tops[h] for h in range(2)]
+        top = [top_rows(1, h) for h in range(2)] if i == 0 else None
         got = [dot(r, bi2[1]) + dot(r[:, 0:128], bi[1, 0, 1]) for r in rows]
         values = []
         for h in range(2):
@@ -570,9 +601,7 @@
         for h in range(2):
             keep_turned(values[h], h, at)
 
-    for k, rows in enumerate(in_two(256)):
-        got = dot3((cyi[0, rows], cyi[1, rows]), (zs[0], zs[1]))
-        s2[1, k] = encode(got[:, 0:128], got[:, 128:256])
+    back_in_y(1)
     exchange(*copies_of(1), part=slice(0, NEXT))
     exchange(*copies_of(0), part=slice(FAR, None))
     exchange(*copies_of(1), part=slice(NEXT, None))
@@ -718,12 +747,14 @@
 
 
 def finish(field_x, field_y, force, sums, out_x, out_y, out_force, energy, overflow, small, sem):
+    pairs = ((field_x, out_x), (field_y, out_y), (force, out_force), (small.at[0], energy), (small.at[1], overflow))
+    copies = [pltpu.make_async_copy(src, dst, sem.at[k]) for k, (src, dst) in enumerate(pairs)]
+    for copy in copies[:3]:
+        copy.start()
     row = sums[...]
     small[0] = row[:, 2:3]
     small[1] = row[:, 0:1] / row[:, 1:2]
-    pairs = ((field_x, out_x), (field_y, out_y), (force, out_force), (small.at[0], energy), (small.at[1], overflow))
-    copies = [pltpu.make_async_copy(src, dst, sem.at[k]) for k, (src, dst) in enumerate(pairs)]
-    for copy in copies:
+    for copy in copies[3:]:
         copy.start()
     for copy in copies:
         copy.wait()
@@ -740,7 +771,7 @@
         V((4, 5, 4, 128), I32),
         V((4, 2, CELLS_DEV), F32),
         V((4, 256, 512), BF),
-        V((2, 512, 512), BF),
+        V((3, 512, 512), BF),
         V((4, 32, CELLS_DEV), F32),
         V((512, 256), F32),
         V((2, 512, 256), BF),
@@ -748,7 +779,6 @@
         V((2, 128, 128), I32),
         V((512, 256), F32),
         V((2, 512, 256), BF),
-        V((2, 16, 256), F32),
         V((512, 128), F32),
         V((512, 128), F32),
         V((256, 128), F32),
@@ -763,6 +793,7 @@
         V((2, 1, 128), F32),
         V((2, 2, 2, 128, 256), BF),
         V((2, 256, 256), BF),
+        V((2, 256, 256), BF),
         V((2, 16, 128), F32),
         V((2, 512, 256), BF),
         V((2, 256, 512), BF),
@@ -771,7 +802,7 @@
         V((2, 2, 2, 128, 256), BF),
         V((2, 256, 256), BF),
         D((11,)), D((6,)),
-        pltpu.SemaphoreType.REGULAR,
+        pltpu.SemaphoreType.REGULAR((2,)),
         D((4,)), D((2, 4)),
         D, D((2,)), D((2,)), D((2,)),
         D((3,)), D((2,)),

time: 40.7 us -> 39.8 us (0.978)
  Pallas kernels: 40 us -> 39.1 us
    pallas_call x1, Pallas kernels: 39.1 us -> 38.2 us  [body(): pl.pallas_call(kernel, out_shape=(V(field, F32), V(field, F32), V((2, CEL...]
where the time goes in v5:
time: 39.8 us; the launch traced here: 39.7 us
  Pallas kernels  39.1 us (98%)
  between operations  0.64 us (2%)
    pallas_call x1, Pallas kernels, body(): pl.pallas_call(kernel, out_shape=(V(field, F32), V(field, F32), V((2, CEL...  38.2 us
    pallas_call x1, Pallas kernels, body(): pl.pallas_call(finish, out_shape=(S(field, F32), S(field, F32), S((2, CEL...  0.84 us

profile of v5, /device:TPU:1, one launch (start us, length us, event | category | flops | bytes accessed | tf_op | source)
XLA Modules:
  0.0 39.7 jit_solution(7391631094425112426)
XLA Ops:
  0.6 38.2 %placement.1 = (f32[4,8,2048]{2,1,0:T(8,128)S(1)}, f32[4,8,2048]{2,1,0:T(8,128)S(1)}, f32[2,512]{1,0:T(2,128)S(1)}, f32[1,128]{1,0:T(1,128)S(1)}) custom-call(s32[4,128]{1,0:T(4,128)} %bitcast.7, s32[4,128]{1,0:T(4,128)} %bitcast.8, s32[4,128]{1,0:T(4,128)} %bitcast.9, s32[4,128]{1,0:T(4,128)} %bitcast.10, s32[4,128]{1,0:T(4,128)} %bitcast.11, ...), custom_call_target="tpu_custom_call" | custom-call | tf_op jit(solution)/shard_map/placement/pallas_call | solution.py:812
  38.9 0.8 %finish.1 = (f32[4,8,2048]{2,1,0:T(8,128)}, f32[4,8,2048]{2,1,0:T(8,128)}, f32[2,512]{1,0:T(2,128)}, f32[1,1]{1,0:T(1,128)}, f32[1,1]{1,0:T(1,128)}) custom-call(f32[4,8,2048]{2,1,0:T(8,128)S(1)} %get-tuple-element.14.field_x, f32[4,8,2048]{2,1,0:T(8,128)S(1)} %get-tuple-element.15.field_y, f32[2,512]{1,0:T(2,128)S(1)} %get-tuple-element.16.force, ...), custom_call_target="tpu_custom_call" | custom-call | tf_op jit(solution)/shard_map/finish/pallas_call | solution.py:824

commit v6 on v5

--- a/solution.py
+++ b/solution.py
@@ -20,6 +20,8 @@
 STEP = math.pi / M
 FAR = 98
 NEXT = 14
+NEAR = 1
+LEAD = 4
 
 
 def c_add(x,y): return (x[0]+y[0], x[1]+y[1])
@@ -220,6 +222,22 @@
     return [slice(base + k * count // 2, base + (k + 1) * count // 2) for k in range(2)]
 
 
+@functools.lru_cache(None)
+def first_devices():
+    def reach(value, count):
+        return min(value, count - value)
+
+    found = []
+    for slab in range(SLABS):
+        for cell in range(2):
+            y, x, z = slab // 32, slab // 8 % 4, slab // 2 % 4 * 2 + cell
+            plane = reach(y, 4) + reach(x, 4)
+            if reach(y, 4) + min(x, 1) + (0 if z < 3 else 3 if z == 3 else reach(z, 8)) <= NEAR:
+                own = slab in (1, 2) and (slab, cell) != (2, 1)
+                found.append((0 if own and plane == 0 else 1 + plane + reach(z, 8) - 0.5 * (slab % 2), slab, cell))
+    return [(slab, cell) for _, slab, cell in sorted(found)]
+
+
 def place():
     slab = lax.axis_index("slab")
     cell = lax.axis_index("cell")
@@ -440,6 +458,23 @@
             slab_to = planes[dy][dx] * 8 + (zh * 2 + (core if dc == 0 else 1 - core))
             send(src(slab_to, zl), dst, s_sem, r_sem, (slab_to, zl)).start()
 
+    def reach(value, count):
+        return jnp.minimum(value, count - value)
+
+    y_reach, x_reach = [reach(v, 4) for v in ys], [jnp.minimum(v, 1) for v in xs]
+    z_reach = [jnp.where(v < 3, 0, jnp.where(v == 3, 3, reach(v, 8))) for v in z_there]
+
+    def exchange_rest(src, dst, s_sem, r_sem, part=slice(None)):
+        for dz, dy, dx, dc in send_order()[part]:
+            zh, zl = z_parts[dz]
+            slab_to = planes[dy][dx] * 8 + (zh * 2 + (core if dc == 0 else 1 - core))
+            start = send(src(slab_to, zl), dst, s_sem, r_sem, (slab_to, zl)).start
+            pl.when(y_reach[dy] + x_reach[dx] + z_reach[dz] > NEAR)(start)
+
+    def exchange_first(src, dst, s_sem, r_sem, part=slice(None)):
+        for slab_to, cell_to in first_devices()[part]:
+            pl.when(me != slab_to * 2 + cell_to)(send(src(slab_to, cell_to), dst, s_sem, r_sem, (slab_to, cell_to)).start)
+
     exchange(lambda slab_to, cell_to: s1.at[pl.ds(slab_to * 2 + cell_to, 1)], r1.at[cell, pl.ds(slab, 1)], a1_s, a1_r.at[cell])
     r1[cell, pl.ds(slab, 1), :] = s1[pl.ds(me, 1), :]
 
@@ -585,6 +620,7 @@
     back_in_y(0)
     r2[0, pl.ds(me, 1), :] = s2[0, cell, pl.ds(slab, 1), :]
 
+    exchange_first(*copies_of(0), part=slice(0, LEAD))
     for i in range(2):
         at = 128 * i
         rows = [vs[1, 256 * h + at : 256 * h + at + 128, :] for h in range(2)]
@@ -597,16 +633,13 @@
             if i == 0:
                 value = jnp.concatenate([jnp.where(top_row, top[h], value[0:16]), value[16:]], axis=0)
             values.append(turned(value, c, s))
-        exchange(*copies_of(0), part=slice(FAR // 2 * i, FAR // 2 * i + FAR // 2))
+        count = len(first_devices()) - LEAD
+        exchange_first(*copies_of(0), part=slice(LEAD + count // 2 * i, LEAD + count // 2 if i == 0 else None))
+        exchange_rest(*copies_of(0), part=slice(FAR // 2 * i, FAR // 2 * i + FAR // 2))
         for h in range(2):
             keep_turned(values[h], h, at)
 
     back_in_y(1)
-    exchange(*copies_of(1), part=slice(0, NEXT))
-    exchange(*copies_of(0), part=slice(FAR, None))
-    exchange(*copies_of(1), part=slice(NEXT, None))
-    r2[1, pl.ds(me, 1), :] = s2[1, cell, pl.ds(slab, 1), :]
-
     def total(x):
         return jnp.sum(jnp.sum(x, axis=1, keepdims=True), axis=0, keepdims=True)
 
@@ -617,6 +650,13 @@
     e1[plane] = row
     for i in range(1, 16):
         send(es.at[0], e1.at[plane], e_s.at[0], e_r.at[0], device_at(lax.rem(plane + i, 16), column)).start()
+
+    exchange_first(*copies_of(1))
+    exchange_rest(*copies_of(1), part=slice(0, NEXT))
+    exchange_rest(*copies_of(0), part=slice(FAR, None))
+    exchange_rest(*copies_of(1), part=slice(NEXT, None))
+    r2[1, pl.ds(me, 1), :] = s2[1, cell, pl.ds(slab, 1), :]
+
     def push(slot, f, halves):
         got = dot(fb[f, 0 : 256 * halves], pq[slot])
         for k in range(4):
@@ -677,19 +717,6 @@
         whole.wait_recv()
         whole.wait_send()
 
-    arrived(0)
-    x_gather(0)
-    x_product(0, (0, 1))
-    for half in range(2):
-        x_inverse(0, field_x, half)
-
-    @pl.when(has_prev)
-    def _():
-        for k in range(2):
-            push(2 + k, 0, 1)
-
-    push(other, 0, 2)
-    push(mine, 0, 2)
     sums_wait = send(e1.at[pl.ds(0, 15)], e1.at[pl.ds(0, 15)], e_s.at[0], e_r.at[0], partner)
     sums_wait.wait_recv()
     sums_wait.wait_send()
@@ -698,6 +725,19 @@
     e2[column] = row
     for i in range(1, 16):
         send(es.at[1], e2.at[column], e_s.at[1], e_r.at[1], device_at(plane, lax.rem(column + i, 16))).start()
+    arrived(0)
+    x_gather(0)
+    x_product(0, (0, 1))
+    for half in range(2):
+        x_inverse(0, field_x, half)
+
+    @pl.when(has_prev)
+    def _():
+        for k in range(2):
+            push(2 + k, 0, 1)
+
+    push(other, 0, 2)
+    push(mine, 0, 2)
     arrived(1)
     x_gather(1)
     x_product(1, (0,))

time: 39.8 us -> 37.7 us (0.947)
  Pallas kernels: 39.1 us -> 37 us
    pallas_call x1, Pallas kernels: 38.2 us -> 36.1 us  [body(): pl.pallas_call(kernel, out_shape=(V(field, F32), V(field, F32), V((2, CEL...]
where the time goes in v6:
time: 37.7 us; the launch traced here: 37.6 us
  Pallas kernels  37 us (98%)
  between operations  0.64 us (2%)
    pallas_call x1, Pallas kernels, body(): pl.pallas_call(kernel, out_shape=(V(field, F32), V(field, F32), V((2, CEL...  36.1 us
    pallas_call x1, Pallas kernels, body(): pl.pallas_call(finish, out_shape=(S(field, F32), S(field, F32), S((2, CEL...  0.84 us

profile of v6, /device:TPU:1, one launch (start us, length us, event | category | flops | bytes accessed | tf_op | source)
XLA Modules:
  0.0 37.6 jit_solution(579204177734885172)
XLA Ops:
  0.6 36.1 %placement.1 = (f32[4,8,2048]{2,1,0:T(8,128)S(1)}, f32[4,8,2048]{2,1,0:T(8,128)S(1)}, f32[2,512]{1,0:T(2,128)S(1)}, f32[1,128]{1,0:T(1,128)S(1)}) custom-call(s32[4,128]{1,0:T(4,128)} %bitcast.7, s32[4,128]{1,0:T(4,128)} %bitcast.8, s32[4,128]{1,0:T(4,128)} %bitcast.9, s32[4,128]{1,0:T(4,128)} %bitcast.10, s32[4,128]{1,0:T(4,128)} %bitcast.11, ...), custom_call_target="tpu_custom_call" | custom-call | tf_op jit(solution)/shard_map/placement/pallas_call | solution.py:852
  36.8 0.8 %finish.1 = (f32[4,8,2048]{2,1,0:T(8,128)}, f32[4,8,2048]{2,1,0:T(8,128)}, f32[2,512]{1,0:T(2,128)}, f32[1,1]{1,0:T(1,128)}, f32[1,1]{1,0:T(1,128)}) custom-call(f32[4,8,2048]{2,1,0:T(8,128)S(1)} %get-tuple-element.14.field_x, f32[4,8,2048]{2,1,0:T(8,128)S(1)} %get-tuple-element.15.field_y, f32[2,512]{1,0:T(2,128)S(1)} %get-tuple-element.16.force, ...), custom_call_target="tpu_custom_call" | custom-call | tf_op jit(solution)/shard_map/finish/pallas_call | solution.py:864

commit v7 on v6

--- a/solution.py
+++ b/solution.py
@@ -416,15 +416,11 @@
                 for k in range(2):
                     zs[k, at, 128 * part : 128 * part + 128] = parts[k]
 
-        def product(rows, kind):
-            got = dot(zs[0, rows], wt[kind])
-            return got[:, 0:128] + (got[:, 128:256] + dot(zs[1, rows], wt[kind, :, 0:128]))
-
-        for rows in in_two(256, 256 * half):
-            gs[rows] = product(rows, 0)
-        first = slice(256 * half, 256 * half + 16)
-        gs[first] = product(first, 1)
         return excess, area
+
+    def x_product_forward(rows, kind):
+        got = dot(zs[0, rows], wt[kind])
+        return got[:, 0:128] + (got[:, 128:256] + dot(zs[1, rows], wt[kind, :, 0:128]))
 
     fetched[0].wait()
     fetched[1].wait()
@@ -440,6 +436,11 @@
             d2[rows] += dot_nt(ym[1, rows], pq[2]) + dot_nt(ym[2, rows], pq[3])
 
     excess, area = x_forward(0, excess, area)
+    for rows in in_two(512):
+        gs[rows] = x_product_forward(rows, 0)
+    for half in range(2):
+        first = slice(256 * half, 256 * half + 16)
+        gs[first] = x_product_forward(first, 1)
     tiles = []
     for t in range(4):
         rows = [gs[256 * half + 16 * kap : 256 * half + 16 * kap + 16] for kap in range(4 * t, 4 * t + 4) for half in range(2)]
@@ -640,6 +641,7 @@
             keep_turned(values[h], h, at)
 
     back_in_y(1)
+    exchange_first(*copies_of(1))
     def total(x):
         return jnp.sum(jnp.sum(x, axis=1, keepdims=True), axis=0, keepdims=True)
 
@@ -650,8 +652,6 @@
     e1[plane] = row
     for i in range(1, 16):
         send(es.at[0], e1.at[plane], e_s.at[0], e_r.at[0], device_at(lax.rem(plane + i, 16), column)).start()
-
-    exchange_first(*copies_of(1))
     exchange_rest(*copies_of(1), part=slice(0, NEXT))
     exchange_rest(*copies_of(0), part=slice(FAR, None))
     exchange_rest(*copies_of(1), part=slice(NEXT, None))
@@ -747,7 +747,6 @@
     def _():
         for k in range(2):
             push(2 + k, 1, 1)
-        for k in range(2):
             give_back(2 + k, (slab - 1, k), 1 + k, 1).start()
 
     x_product(1, (1,))

time: 37.7 us -> 37.6 us (level)
  no operation moved by 1% of the time
where the time goes in v7:
time: 37.6 us; the launch traced here: 37.5 us
  Pallas kernels  36.8 us (98%)
  between operations  0.64 us (2%)
    pallas_call x1, Pallas kernels, body(): pl.pallas_call(kernel, out_shape=(V(field, F32), V(field, F32), V((2, CEL...  36 us
    pallas_call x1, Pallas kernels, body(): pl.pallas_call(finish, out_shape=(S(field, F32), S(field, F32), S((2, CEL...  0.84 us

profile of v7, /device:TPU:1, one launch (start us, length us, event | category | flops | bytes accessed | tf_op | source)
XLA Modules:
  0.0 37.5 jit_solution(548907325801301048)
XLA Ops:
  0.6 36.0 %placement.1 = (f32[4,8,2048]{2,1,0:T(8,128)S(1)}, f32[4,8,2048]{2,1,0:T(8,128)S(1)}, f32[2,512]{1,0:T(2,128)S(1)}, f32[1,128]{1,0:T(1,128)S(1)}) custom-call(s32[4,128]{1,0:T(4,128)} %bitcast.7, s32[4,128]{1,0:T(4,128)} %bitcast.8, s32[4,128]{1,0:T(4,128)} %bitcast.9, s32[4,128]{1,0:T(4,128)} %bitcast.10, s32[4,128]{1,0:T(4,128)} %bitcast.11, ...), custom_call_target="tpu_custom_call" | custom-call | tf_op jit(solution)/shard_map/placement/pallas_call | solution.py:851
  36.6 0.8 %finish.1 = (f32[4,8,2048]{2,1,0:T(8,128)}, f32[4,8,2048]{2,1,0:T(8,128)}, f32[2,512]{1,0:T(2,128)}, f32[1,1]{1,0:T(1,128)}, f32[1,1]{1,0:T(1,128)}) custom-call(f32[4,8,2048]{2,1,0:T(8,128)S(1)} %get-tuple-element.14.field_x, f32[4,8,2048]{2,1,0:T(8,128)S(1)} %get-tuple-element.15.field_y, f32[2,512]{1,0:T(2,128)S(1)} %get-tuple-element.16.force, ...), custom_call_target="tpu_custom_call" | custom-call | tf_op jit(solution)/shard_map/finish/pallas_call | solution.py:863

commit v8 on v7

--- a/solution.py
+++ b/solution.py
@@ -737,7 +737,6 @@
             push(2 + k, 0, 1)
 
     push(other, 0, 2)
-    push(mine, 0, 2)
     arrived(1)
     x_gather(1)
     x_product(1, (0,))
@@ -753,7 +752,8 @@
     x_inverse(1, field_y, 1)
     push(other, 1, 2)
     give_back(other, partner, 0, 0).start()
-    push(mine, 1, 2)
+    for f in range(2):
+        push(mine, f, 2)
 
     @pl.when(jnp.logical_not(has_next))
     def _():

time: 37.6 us -> 37.6 us (level)
  no operation moved by 1% of the time
where the time goes in v8:
time: 37.6 us; the launch traced here: 37.5 us
  Pallas kernels  36.8 us (98%)
  between operations  0.64 us (2%)
    pallas_call x1, Pallas kernels, body(): pl.pallas_call(kernel, out_shape=(V(field, F32), V(field, F32), V((2, CEL...  36 us
    pallas_call x1, Pallas kernels, body(): pl.pallas_call(finish, out_shape=(S(field, F32), S(field, F32), S((2, CEL...  0.84 us

profile of v8, /device:TPU:1, one launch (start us, length us, event | category | flops | bytes accessed | tf_op | source)
XLA Modules:
  0.0 37.5 jit_solution(16637286530799937783)
XLA Ops:
  0.6 36.0 %placement.1 = (f32[4,8,2048]{2,1,0:T(8,128)S(1)}, f32[4,8,2048]{2,1,0:T(8,128)S(1)}, f32[2,512]{1,0:T(2,128)S(1)}, f32[1,128]{1,0:T(1,128)S(1)}) custom-call(s32[4,128]{1,0:T(4,128)} %bitcast.7, s32[4,128]{1,0:T(4,128)} %bitcast.8, s32[4,128]{1,0:T(4,128)} %bitcast.9, s32[4,128]{1,0:T(4,128)} %bitcast.10, s32[4,128]{1,0:T(4,128)} %bitcast.11, ...), custom_call_target="tpu_custom_call" | custom-call | tf_op jit(solution)/shard_map/placement/pallas_call | solution.py:851
  36.6 0.8 %finish.1 = (f32[4,8,2048]{2,1,0:T(8,128)}, f32[4,8,2048]{2,1,0:T(8,128)}, f32[2,512]{1,0:T(2,128)}, f32[1,1]{1,0:T(1,128)}, f32[1,1]{1,0:T(1,128)}) custom-call(f32[4,8,2048]{2,1,0:T(8,128)S(1)} %get-tuple-element.14.field_x, f32[4,8,2048]{2,1,0:T(8,128)S(1)} %get-tuple-element.15.field_y, f32[2,512]{1,0:T(2,128)S(1)} %get-tuple-element.16.force, ...), custom_call_target="tpu_custom_call" | custom-call | tf_op jit(solution)/shard_map/finish/pallas_call | solution.py:863
